TPU v7x, 256 devices: a whole 4x4x8 slice. The times are simulated.
256 devices in a mesh: gz: 64 (over x, z_hi, y), xy: 4 (over z_lo, core).
Axes of the slice: x: 4, y: 4, z: 8 (z_hi: 4, z_lo: 2; z = z_hi * 2 + z_lo), core: 2. Of those that a mesh axis runs over, the one named last changes fastest.
Arguments:
- patches: bfloat16 [64, 8, 16, 128, 128], P('gz', 'xy'), may hold values from -6 to 6
- peak_offsets: int32 [64, 6, 8, 16], P('gz', None, 'xy'), may hold values from -4 to 4
- valid_masks: int32 [64, 3, 8, 16], P('gz', None, 'xy'), may hold values 0 or 1
- initial_positions: float32 [2, 64, 128, 256], P(None, 'gz', 'xy'), may hold values from -40 to 40
Outputs:
- positions: float32 [2, 64, 128, 256], P(None, 'gz', 'xy')
- targets: float32 [64, 6, 8, 16], P('gz', None, 'xy')
- surfaces: bfloat16 [64, 3, 8, 16, 128, 128], P('gz', None, 'xy')
- force_rms: float32 [4], replicated
All inputs are finite; a program needn't handle non-finite values. No bound on the sum of `valid_masks` on one device may be relied on, other than what follows from the above.
Results may differ from a plain program's by a relative error of at most 0.0091.
Values may be sent and summed in bfloat16 or wider, within the bound.
A program may use at most 64 MiB of HBM per device.

v0:
```python
import math

import jax
import jax.numpy as jnp
from jax import lax
from jax.sharding import Mesh
from jax.sharding import PartitionSpec as P

SUB = 16
ITERS = 4
GZ = ("gz_0", "gz_1", "gz_2")
XY = ("xy_0", "xy_1")
GZ_XY = ("gz_0", "gz_1", "gz_2", "xy_0", "xy_1")


lattice_stiff = 0.5
clip_level = 5.0
step_size = 0.2
floor_ratio = 0.4
tiny_eps = 1e-06


def from_behind(array, axis, by):
    count = lax.axis_size(axis)
    pairs = [(i, i + by) for i in range(count) if 0 <= i + by < count]
    return lax.ppermute(array, axis, pairs)


def extended(block, sides, width):
    for axis, dim in sides:
        count = lax.axis_size(axis)
        forward = [(i, i + 1) for i in range(count - 1)]
        backward = [(target, source) for source, target in forward]
        low = lax.ppermute(
            lax.slice_in_dim(block, block.shape[dim] - width, None, axis=dim), axis, forward
        )
        high = lax.ppermute(lax.slice_in_dim(block, 0, width, axis=dim), axis, backward)
        block = jnp.concatenate([low, block, high], axis=dim)
    return block


def over_axes(array, axes):
    for axis in axes:
        array = lax.psum(array, axis)
    return array


def dft_tables(length):
    series = jnp.arange(length, dtype=jnp.int32)
    product = series[:, None] * series[None, :] % length
    angles = 2.0 * math.pi / length * product.astype(jnp.float32)
    return (jnp.cos(angles).astype(jnp.bfloat16), jnp.sin(angles).astype(jnp.bfloat16))


def right_product(left, table):
    return jnp.einsum("pab,bk->pak", left, table, preferred_element_type=jnp.float32)


def left_product(table, right):
    return jnp.einsum("ja,pak->pjk", table, right, preferred_element_type=jnp.float32)


def spectrum(tiles, cosine, sine):
    row_cos = right_product(tiles, cosine).astype(jnp.bfloat16)
    row_sin = right_product(tiles, sine).astype(jnp.bfloat16)
    real = left_product(cosine, row_cos) - left_product(sine, row_sin)
    imag = -(left_product(sine, row_cos) + left_product(cosine, row_sin))
    return (real, imag)


def correlate(first, second, cosine, sine, length):
    cross_real = (first[0] * second[0] + first[1] * second[1]).astype(jnp.bfloat16)
    cross_imag = (first[0] * second[1] - first[1] * second[0]).astype(jnp.bfloat16)
    half_real = (right_product(cross_real, cosine) - right_product(cross_imag, sine)).astype(
        jnp.bfloat16
    )
    half_imag = (right_product(cross_real, sine) + right_product(cross_imag, cosine)).astype(
        jnp.bfloat16
    )
    whole = left_product(cosine, half_real) - left_product(sine, half_imag)
    return whole / float(length * length)


def refine(corr, shift_rows, shift_cols, length):
    series = jnp.arange(length, dtype=jnp.int32)
    taps = jnp.arange(3, dtype=jnp.int32) - 1
    row_index = (shift_rows[:, None] + taps[None, :] + length) % length
    col_index = (shift_cols[:, None] + taps[None, :] + length) % length
    row_pick = (series[None, None, :] == row_index[:, :, None]).astype(jnp.float32)
    col_pick = (series[None, None, :] == col_index[:, :, None]).astype(jnp.float32)
    partial_rows = jnp.einsum("pta,pab->ptb", row_pick, corr)
    values = jnp.einsum("ptb,psb->pts", partial_rows, col_pick)
    floor_value = floor_ratio * length
    along_rows = values[:, :, 1]
    along_cols = values[:, 1, :]
    sub_rows = (along_rows[:, 2] - along_rows[:, 0]) / jnp.maximum(
        jnp.sum(jnp.abs(along_rows), axis=1), floor_value
    )
    sub_cols = (along_cols[:, 2] - along_cols[:, 0]) / jnp.maximum(
        jnp.sum(jnp.abs(along_cols), axis=1), floor_value
    )
    return (shift_rows.astype(jnp.float32) + sub_rows, shift_cols.astype(jnp.float32) + sub_cols)


def expand_nodes(array, axis):
    return jnp.repeat(jnp.repeat(array, SUB, axis=axis), SUB, axis=axis + 1)


def local(patches, peak_offsets, valid_masks, initial_positions):
    length = patches.shape[-1]
    rows_dev = patches.shape[1]
    columns = patches.shape[2]
    tiles_count = rows_dev * columns
    cosine, sine = dft_tables(length)
    own = spectrum(patches.reshape(tiles_count, length, length), cosine, sine)
    offsets = peak_offsets.reshape(6, tiles_count)
    results = []
    maps = []
    for distance in range(1, 4):
        other_tiles = from_behind(patches, GZ, -distance)
        other = spectrum(other_tiles.reshape(tiles_count, length, length), cosine, sine)
        corr = correlate(own, other, cosine, sine, length)
        maps.append(corr.astype(jnp.bfloat16).reshape(rows_dev, columns, length, length))
        rows_target, cols_target = refine(
            corr, offsets[2 * distance - 2], offsets[2 * distance - 1], length
        )
        results.append(rows_target)
        results.append(cols_target)
    targets = jnp.stack(results).reshape(1, 6, rows_dev, columns)
    surfaces = jnp.stack(maps).reshape(1, 3, rows_dev, columns, length, length)
    depth_count = lax.axis_size(GZ)
    depth_index = lax.axis_index(GZ)
    tile_index = lax.axis_index(XY)
    tile_count = lax.axis_size(XY)
    weights = []
    vectors = []
    lower_weights = []
    lower_vectors = []
    for distance in range(1, 4):
        live = (depth_index + distance < depth_count).astype(jnp.float32)
        weight = valid_masks[:, distance - 1].astype(jnp.float32) * (1.0 / distance) * live
        vector = jnp.stack([targets[:, 2 * distance - 2], targets[:, 2 * distance - 1]], axis=0)
        vector_low, weight_low = from_behind((vector, weight), GZ, distance)
        weights.append(expand_nodes(weight, 1))
        vectors.append(expand_nodes(vector, 2))
        lower_weights.append(expand_nodes(weight_low, 1))
        lower_vectors.append(expand_nodes(vector_low, 2))
    count = 2.0 * depth_count * tile_count * initial_positions.shape[2] * initial_positions.shape[3]
    positions = initial_positions
    norms = []
    for iteration in range(ITERS):
        padded = extended(positions.astype(jnp.bfloat16), ((XY, 2),), 1).astype(positions.dtype)
        top_row = jnp.where(tile_index == 0, positions[:, :, :1], padded[:, :, :1])
        bottom_row = jnp.where(
            tile_index == tile_count - 1, positions[:, :, -1:], padded[:, :, -1:]
        )
        upper_rows = jnp.concatenate([top_row, positions[:, :, :-1]], axis=2)
        lower_rows = jnp.concatenate([positions[:, :, 1:], bottom_row], axis=2)
        edged = jnp.pad(positions, ((0, 0), (0, 0), (0, 0), (1, 1)), mode="edge")
        lattice = (
            upper_rows + lower_rows + edged[:, :, :, :-2] + edged[:, :, :, 2:] - 4.0 * positions
        )
        force = lattice_stiff * lattice
        climbing = positions
        sinking = positions
        for distance in range(1, 4):
            climbing = from_behind(climbing.astype(jnp.bfloat16), GZ, -1).astype(climbing.dtype)
            sinking = from_behind(sinking.astype(jnp.bfloat16), GZ, 1).astype(sinking.dtype)
            force = force + weights[distance - 1] * (climbing - positions - vectors[distance - 1])
            force = force - lower_weights[distance - 1] * (
                positions - sinking - lower_vectors[distance - 1]
            )
        total = over_axes(jnp.sum(force * force), GZ_XY)
        rms = jnp.sqrt(total / count + tiny_eps)
        factor = jnp.minimum(1.0, clip_level / rms)
        positions = positions + step_size * factor * force
        norms.append(rms)
    return (positions, targets, surfaces, jnp.stack(norms))


def solution(mesh):
    split = Mesh(mesh.devices.reshape(4, 4, 4, 2, 2), ("gz_0", "gz_1", "gz_2", "xy_0", "xy_1"))
    placed = (
        P(GZ, XY, None, None, None),
        P(GZ, None, XY, None),
        P(GZ, None, XY, None),
        P(None, GZ, XY, None),
    )
    return jax.shard_map(
        local,
        mesh=split,
        in_specs=placed,
        out_specs=(
            P(None, GZ, XY, None),
            P(GZ, None, XY, None),
            P(GZ, None, XY, None, None, None),
            P(),
        ),
        check_vma=False,
    )
```

profile of v0, /device:TPU:1, one launch (start us, length us, event | category | flops | bytes accessed | tf_op | source)
XLA Modules:
  0.0 543.9 jit_solution(4362355122713396732)
XLA Ops:
  6.1 5.2 collective-permute-start.5
  25.6 10.0 %collective-permute-start.9 = (f32[1,2,16]{2,1,0:T(2,128)S(1)}, f32[1,2,16]{2,1,0:T(2,128)S(1)}, u32[]{:S(2)}, u32[]{:S(2)}) collective-permute-start(f32[1,2,16]{2,1,0:T(2,128)S(1)} %get-tuple-element.92), channel_id=1, source_target_pairs={{0,8},{4,12},{8,16},{12,20},{16,24},{20,28},{24,32},{28,36},{32,40... | collective-permute-start | bytes 392 | tf_op jit(solution)/shard_map/ppermute | solution.py:26
  36.4 6.4 %collective-permute-start.14 = (f32[1,2,16]{2,1,0:T(2,128)S(1)}, f32[1,2,16]{2,1,0:T(2,128)S(1)}, u32[]{:S(2)}, u32[]{:S(2)}) collective-permute-start(f32[1,2,16]{2,1,0:T(2,128)S(1)} %get-tuple-element.91), channel_id=1, source_target_pairs={{0,12},{4,16},{8,20},{12,24},{16,28},{20,32},{24,36},{28,40},{32,4... | collective-permute-start | bytes 392 | tf_op jit(solution)/shard_map/ppermute | solution.py:26
  43.4 29.5 %collective-permute-start = (bf16[2,1,1,256]{3,2,1,0:T(2,128)(2,1)S(1)}, bf16[2,1,1,256]{3,2,1,0:T(2,128)(2,1)S(1)}, u32[]{:S(2)}, u32[]{:S(2)}) collective-permute-start(bf16[2,1,1,256]{3,2,1,0:T(2,128)(2,1)S(1)} %get-tuple-element.82), channel_id=1, source_target_pairs={{0,1},{1,2},{2,3},{4,5},{5,6},{6,7},{8,9},{9,10},{10,11},{12,13},{... | collective-permute-start | bytes 3080 | tf_op jit(solution)/shard_map/ppermute | solution.py:34
  81.9 6.0 %collective-permute-start.10 = (bf16[2,1,32,256]{3,2,1,0:T(8,128)(2,1)}, bf16[2,1,32,256]{3,2,1,0:T(8,128)(2,1)}, u32[]{:S(2)}, u32[]{:S(2)}) collective-permute-start(bf16[2,1,32,256]{3,2,1,0:T(8,128)(2,1)} %collective-permute-done.5), channel_id=1, source_target_pairs={{0,4},{4,8},{8,12},{12,16},{16,20},{20,24},{24,28},{28,32},{32,36}... | collective-permute-start | bytes 98312 | tf_op jit(solution)/shard_map/ppermute | solution.py:26
  88.4 34.0 %collective-permute-done.7 = bf16[2,1,32,256]{3,2,1,0:T(8,128)(2,1)} collective-permute-done((bf16[2,1,32,256]{3,2,1,0:T(8,128)(2,1)}, bf16[2,1,32,256]{3,2,1,0:T(8,128)(2,1)}, u32[]{:S(2)}, u32[]{:S(2)}) %collective-permute-start.7) | collective-permute-done | bytes 32800 | tf_op jit(solution)/shard_map/ppermute | solution.py:26
  198.8 6.9 %collective-permute-start.6 = (f32[2,1,2,16]{3,2,1,0:T(2,128)S(1)}, f32[2,1,2,16]{3,2,1,0:T(2,128)S(1)}, u32[]{:S(2)}, u32[]{:S(2)}) collective-permute-start(f32[2,1,2,16]{3,2,1,0:T(2,128)S(1)} %get-tuple-element.97), channel_id=1, source_target_pairs={{0,4},{4,8},{8,12},{12,16},{16,20},{20,24},{24,28},{28,32},{32,36}... | collective-permute-start | bytes 776 | tf_op jit(solution)/shard_map/ppermute | solution.py:26
  206.8 25.7 %collective-permute-start.11 = (f32[2,1,2,16]{3,2,1,0:T(2,128)S(1)}, f32[2,1,2,16]{3,2,1,0:T(2,128)S(1)}, u32[]{:S(2)}, u32[]{:S(2)}) collective-permute-start(f32[2,1,2,16]{3,2,1,0:T(2,128)S(1)} %get-tuple-element.99), channel_id=1, source_target_pairs={{0,8},{4,12},{8,16},{12,20},{16,24},{20,28},{24,32},{28,36},{32,40... | collective-permute-start | bytes 776 | tf_op jit(solution)/shard_map/ppermute | solution.py:26
  240.7 20.3 %psum.140 = f32[]{:T(128)} all-reduce(f32[]{:T(128)} %get-tuple-element.40), channel_id=1, replica_groups=mesh['gz_0'=4,'gz_1'=4,'gz_2'=4,'xy_0'=2,'xy_1'=2] {'gz_0'}, use_global_device_ids=true, to_apply=%region_7.8 | all-reduce | flops 1 | bytes 8 | tf_op jit(solution)/shard_map/psum | solution.py:44
  260.9 9.2 %psum.141 = f32[]{:T(128)} all-reduce(f32[]{:T(128)} %psum.140), channel_id=1, replica_groups=mesh['gz_0'=4,'gz_1'=4,'gz_2'=4,'xy_0'=2,'xy_1'=2] {'gz_1'}, use_global_device_ids=true, to_apply=%region_8.9 | all-reduce | flops 1 | bytes 8 | tf_op jit(solution)/shard_map/psum | solution.py:44
  270.2 6.6 %psum.142 = f32[]{:T(128)} all-reduce(f32[]{:T(128)} %psum.141), channel_id=1, replica_groups=mesh['gz_0'=4,'gz_1'=4,'gz_2'=4,'xy_0'=2,'xy_1'=2] {'gz_2'}, use_global_device_ids=true, to_apply=%region_9.10 | all-reduce | flops 1 | bytes 8 | tf_op jit(solution)/shard_map/psum | solution.py:44
  281.4 10.7 %psum.144 = f32[]{:T(128)} all-reduce(f32[]{:T(128)} %psum.143), channel_id=1, replica_groups=mesh['gz_0'=4,'gz_1'=4,'gz_2'=4,'xy_0'=2,'xy_1'=2] {'xy_1'}, use_global_device_ids=true, to_apply=%region_11.12 | all-reduce | flops 1 | bytes 8 | tf_op jit(solution)/shard_map/psum | solution.py:44
  315.3 24.1 %psum.145 = f32[]{:T(128)} all-reduce(f32[]{:T(128)} %get-tuple-element.36), channel_id=1, replica_groups=mesh['gz_0'=4,'gz_1'=4,'gz_2'=4,'xy_0'=2,'xy_1'=2] {'gz_0'}, use_global_device_ids=true, to_apply=%region_13.14 | all-reduce | flops 1 | bytes 8 | tf_op jit(solution)/shard_map/psum | solution.py:44
  339.4 7.5 %psum.146 = f32[]{:T(128)} all-reduce(f32[]{:T(128)} %psum.145), channel_id=1, replica_groups=mesh['gz_0'=4,'gz_1'=4,'gz_2'=4,'xy_0'=2,'xy_1'=2] {'gz_1'}, use_global_device_ids=true, to_apply=%region_14.15 | all-reduce | flops 1 | bytes 8 | tf_op jit(solution)/shard_map/psum | solution.py:44
  346.9 6.6 %psum.147 = f32[]{:T(128)} all-reduce(f32[]{:T(128)} %psum.146), channel_id=1, replica_groups=mesh['gz_0'=4,'gz_1'=4,'gz_2'=4,'xy_0'=2,'xy_1'=2] {'gz_2'}, use_global_device_ids=true, to_apply=%region_15.16 | all-reduce | flops 1 | bytes 8 | tf_op jit(solution)/shard_map/psum | solution.py:44
  357.9 11.4 %psum.149 = f32[]{:T(128)} all-reduce(f32[]{:T(128)} %psum.148), channel_id=1, replica_groups=mesh['gz_0'=4,'gz_1'=4,'gz_2'=4,'xy_0'=2,'xy_1'=2] {'xy_1'}, use_global_device_ids=true, to_apply=%region_17.18 | all-reduce | flops 1 | bytes 8 | tf_op jit(solution)/shard_map/psum | solution.py:44
  394.5 27.3 %psum.150 = f32[]{:T(128)} all-reduce(f32[]{:T(128)} %get-tuple-element.32), channel_id=1, replica_groups=mesh['gz_0'=4,'gz_1'=4,'gz_2'=4,'xy_0'=2,'xy_1'=2] {'gz_0'}, use_global_device_ids=true, to_apply=%region_19.20 | all-reduce | flops 1 | bytes 8 | tf_op jit(solution)/shard_map/psum | solution.py:44
  421.8 7.5 %psum.151 = f32[]{:T(128)} all-reduce(f32[]{:T(128)} %psum.150), channel_id=1, replica_groups=mesh['gz_0'=4,'gz_1'=4,'gz_2'=4,'xy_0'=2,'xy_1'=2] {'gz_1'}, use_global_device_ids=true, to_apply=%region_20.21 | all-reduce | flops 1 | bytes 8 | tf_op jit(solution)/shard_map/psum | solution.py:44
  429.3 6.6 %psum.152 = f32[]{:T(128)} all-reduce(f32[]{:T(128)} %psum.151), channel_id=1, replica_groups=mesh['gz_0'=4,'gz_1'=4,'gz_2'=4,'xy_0'=2,'xy_1'=2] {'gz_2'}, use_global_device_ids=true, to_apply=%region_21.22 | all-reduce | flops 1 | bytes 8 | tf_op jit(solution)/shard_map/psum | solution.py:44
  440.3 11.4 %psum.154 = f32[]{:T(128)} all-reduce(f32[]{:T(128)} %psum.153), channel_id=1, replica_groups=mesh['gz_0'=4,'gz_1'=4,'gz_2'=4,'xy_0'=2,'xy_1'=2] {'xy_1'}, use_global_device_ids=true, to_apply=%region_23.24 | all-reduce | flops 1 | bytes 8 | tf_op jit(solution)/shard_map/psum | solution.py:44
  476.9 27.3 %psum.155 = f32[]{:T(128)} all-reduce(f32[]{:T(128)} %get-tuple-element.28), channel_id=1, replica_groups=mesh['gz_0'=4,'gz_1'=4,'gz_2'=4,'xy_0'=2,'xy_1'=2] {'gz_0'}, use_global_device_ids=true, to_apply=%region_25.26 | all-reduce | flops 1 | bytes 8 | tf_op jit(solution)/shard_map/psum | solution.py:44
  505.5 7.5 %psum.156 = f32[]{:T(128)} all-reduce(f32[]{:T(128)} %psum.155), channel_id=1, replica_groups=mesh['gz_0'=4,'gz_1'=4,'gz_2'=4,'xy_0'=2,'xy_1'=2] {'gz_1'}, use_global_device_ids=true, to_apply=%region_26.27 | all-reduce | flops 1 | bytes 8 | tf_op jit(solution)/shard_map/psum | solution.py:44
  514.3 6.6 %psum.157 = f32[]{:T(128)} all-reduce(f32[]{:T(128)} %psum.156), channel_id=1, replica_groups=mesh['gz_0'=4,'gz_1'=4,'gz_2'=4,'xy_0'=2,'xy_1'=2] {'gz_2'}, use_global_device_ids=true, to_apply=%region_27.28 | all-reduce | flops 1 | bytes 8 | tf_op jit(solution)/shard_map/psum | solution.py:44
  529.9 11.6 %psum.159 = f32[]{:T(128)} all-reduce(f32[]{:T(128)} %psum.158), channel_id=1, replica_groups=mesh['gz_0'=4,'gz_1'=4,'gz_2'=4,'xy_0'=2,'xy_1'=2] {'xy_1'}, use_global_device_ids=true, to_apply=%region_29.30 | all-reduce | flops 1 | bytes 8 | tf_op jit(solution)/shard_map/psum | solution.py:44
  (311 shorter events, 212.9 us)
Async XLA Ops:
  0.6 127.8 %collective-permute-start.13 = (bf16[1,2,16,128,128]{4,3,2,1,0:T(8,128)(2,1)}, bf16[1,2,16,128,128]{4,3,2,1,0:T(8,128)(2,1)}, u32[]{:S(2)}, u32[]{:S(2)}) collective-permute-start(bf16[1,2,16,128,128]{4,3,2,1,0:T(8,128)(2,1)} %param.4), channel_id=1, source_target_pairs={{12,0},{16,4},{20,8},{24,12},{28,16},{32,20},{36,24},{40,28},{44,3... | collective-permute-start | bytes 3145736 | tf_op jit(solution)/shard_map/ppermute | solution.py:26
  2.1 130.3 %collective-permute-start.8 = (bf16[1,2,16,128,128]{4,3,2,1,0:T(8,128)(2,1)}, bf16[1,2,16,128,128]{4,3,2,1,0:T(8,128)(2,1)}, u32[]{:S(2)}, u32[]{:S(2)}) collective-permute-start(bf16[1,2,16,128,128]{4,3,2,1,0:T(8,128)(2,1)} %param.4), channel_id=1, source_target_pairs={{8,0},{12,4},{16,8},{20,12},{24,16},{28,20},{32,24},{36,28},{40,32... | collective-permute-start | bytes 3145736 | tf_op jit(solution)/shard_map/ppermute | solution.py:26
  4.8 75.7 %collective-permute-start.2 = (bf16[2,1,32,256]{3,2,1,0:T(8,128)(2,1)}, bf16[2,1,32,256]{3,2,1,0:T(8,128)(2,1)}, u32[]{:S(2)}, u32[]{:S(2)}) collective-permute-start(bf16[2,1,32,256]{3,2,1,0:T(8,128)(2,1)} %convert_element_type.496), channel_id=1, source_target_pairs={{4,0},{8,4},{12,8},{16,12},{20,16},{24,20},{28,24},{32,28},{36,32}... | collective-permute-start | bytes 98312 | tf_op jit(solution)/shard_map/ppermute | solution.py:26
  6.1 75.8 %collective-permute-start.5 = (bf16[2,1,32,256]{3,2,1,0:T(8,128)(2,1)}, bf16[2,1,32,256]{3,2,1,0:T(8,128)(2,1)}, u32[]{:S(2)}, u32[]{:S(2)}) collective-permute-start(bf16[2,1,32,256]{3,2,1,0:T(8,128)(2,1)} %convert_element_type.496), channel_id=1, source_target_pairs={{0,4},{4,8},{8,12},{12,16},{16,20},{20,24},{24,28},{28,32},{32,36}... | collective-permute-start | bytes 98312 | tf_op jit(solution)/shard_map/ppermute | solution.py:26
  12.1 13.5 %collective-permute-start.4 = (f32[1,2,16]{2,1,0:T(2,128)S(1)}, f32[1,2,16]{2,1,0:T(2,128)S(1)}, u32[]{:S(2)}, u32[]{:S(2)}) collective-permute-start(f32[1,2,16]{2,1,0:T(2,128)S(1)} %get-tuple-element.93), channel_id=1, source_target_pairs={{0,4},{4,8},{8,12},{12,16},{16,20},{20,24},{24,28},{28,32},{32,36}... | collective-permute-start | bytes 392 | tf_op jit(solution)/shard_map/ppermute | solution.py:26
  25.6 10.7 %collective-permute-start.9 = (f32[1,2,16]{2,1,0:T(2,128)S(1)}, f32[1,2,16]{2,1,0:T(2,128)S(1)}, u32[]{:S(2)}, u32[]{:S(2)}) collective-permute-start(f32[1,2,16]{2,1,0:T(2,128)S(1)} %get-tuple-element.92), channel_id=1, source_target_pairs={{0,8},{4,12},{8,16},{12,20},{16,24},{20,28},{24,32},{28,36},{32,40... | collective-permute-start | bytes 392 | tf_op jit(solution)/shard_map/ppermute | solution.py:26
  43.4 30.2 %collective-permute-start = (bf16[2,1,1,256]{3,2,1,0:T(2,128)(2,1)S(1)}, bf16[2,1,1,256]{3,2,1,0:T(2,128)(2,1)S(1)}, u32[]{:S(2)}, u32[]{:S(2)}) collective-permute-start(bf16[2,1,1,256]{3,2,1,0:T(2,128)(2,1)S(1)} %get-tuple-element.82), channel_id=1, source_target_pairs={{0,1},{1,2},{2,3},{4,5},{5,6},{6,7},{8,9},{9,10},{10,11},{12,13},{... | collective-permute-start | bytes 3080 | tf_op jit(solution)/shard_map/ppermute | solution.py:34
  79.3 56.9 %collective-permute-start.3 = (bf16[1,2,16,128,128]{4,3,2,1,0:T(8,128)(2,1)S(1)}, bf16[1,2,16,128,128]{4,3,2,1,0:T(8,128)(2,1)S(1)}, u32[]{:S(2)}, u32[]{:S(2)}) collective-permute-start(bf16[1,2,16,128,128]{4,3,2,1,0:T(8,128)(2,1)S(1)} %copy-done.7), channel_id=1, source_target_pairs={{4,0},{8,4},{12,8},{16,12},{20,16},{24,20},{28,24},{32,28},{36,32}... | collective-permute-start | bytes 3145736 | tf_op jit(solution)/shard_map/ppermute | solution.py:26
  80.6 41.8 %collective-permute-start.7 = (bf16[2,1,32,256]{3,2,1,0:T(8,128)(2,1)}, bf16[2,1,32,256]{3,2,1,0:T(8,128)(2,1)}, u32[]{:S(2)}, u32[]{:S(2)}) collective-permute-start(bf16[2,1,32,256]{3,2,1,0:T(8,128)(2,1)} %collective-permute-done.2), channel_id=1, source_target_pairs={{4,0},{8,4},{12,8},{16,12},{20,16},{24,20},{28,24},{32,28},{36,32}... | collective-permute-start | bytes 98312 | tf_op jit(solution)/shard_map/ppermute | solution.py:26
  81.9 41.8 %collective-permute-start.10 = (bf16[2,1,32,256]{3,2,1,0:T(8,128)(2,1)}, bf16[2,1,32,256]{3,2,1,0:T(8,128)(2,1)}, u32[]{:S(2)}, u32[]{:S(2)}) collective-permute-start(bf16[2,1,32,256]{3,2,1,0:T(8,128)(2,1)} %collective-permute-done.5), channel_id=1, source_target_pairs={{0,4},{4,8},{8,12},{12,16},{16,20},{20,24},{24,28},{28,32},{32,36}... | collective-permute-start | bytes 98312 | tf_op jit(solution)/shard_map/ppermute | solution.py:26
  122.4 116.6 %collective-permute-start.12 = (bf16[2,1,32,256]{3,2,1,0:T(8,128)(2,1)}, bf16[2,1,32,256]{3,2,1,0:T(8,128)(2,1)}, u32[]{:S(2)}, u32[]{:S(2)}) collective-permute-start(bf16[2,1,32,256]{3,2,1,0:T(8,128)(2,1)} %collective-permute-done.7), channel_id=1, source_target_pairs={{4,0},{8,4},{12,8},{16,12},{20,16},{24,20},{28,24},{32,28},{36,32}... | collective-permute-start | bytes 98312 | tf_op jit(solution)/shard_map/ppermute | solution.py:26
  123.7 115.3 %collective-permute-start.15 = (bf16[2,1,32,256]{3,2,1,0:T(8,128)(2,1)}, bf16[2,1,32,256]{3,2,1,0:T(8,128)(2,1)}, u32[]{:S(2)}, u32[]{:S(2)}) collective-permute-start(bf16[2,1,32,256]{3,2,1,0:T(8,128)(2,1)} %collective-permute-done.10), channel_id=1, source_target_pairs={{0,4},{4,8},{8,12},{12,16},{16,20},{20,24},{24,28},{28,32},{32,36}... | collective-permute-start | bytes 98312 | tf_op jit(solution)/shard_map/ppermute | solution.py:26
  198.8 38.9 %collective-permute-start.6 = (f32[2,1,2,16]{3,2,1,0:T(2,128)S(1)}, f32[2,1,2,16]{3,2,1,0:T(2,128)S(1)}, u32[]{:S(2)}, u32[]{:S(2)}) collective-permute-start(f32[2,1,2,16]{3,2,1,0:T(2,128)S(1)} %get-tuple-element.97), channel_id=1, source_target_pairs={{0,4},{4,8},{8,12},{12,16},{16,20},{20,24},{24,28},{28,32},{32,36}... | collective-permute-start | bytes 776 | tf_op jit(solution)/shard_map/ppermute | solution.py:26
  206.8 31.4 %collective-permute-start.11 = (f32[2,1,2,16]{3,2,1,0:T(2,128)S(1)}, f32[2,1,2,16]{3,2,1,0:T(2,128)S(1)}, u32[]{:S(2)}, u32[]{:S(2)}) collective-permute-start(f32[2,1,2,16]{3,2,1,0:T(2,128)S(1)} %get-tuple-element.99), channel_id=1, source_target_pairs={{0,8},{4,12},{8,16},{12,20},{16,24},{20,28},{24,32},{28,36},{32,40... | collective-permute-start | bytes 776 | tf_op jit(solution)/shard_map/ppermute | solution.py:26
  298.5 15.1 %collective-permute-start.17 = (bf16[2,1,1,256]{3,2,1,0:T(2,128)(2,1)S(1)}, bf16[2,1,1,256]{3,2,1,0:T(2,128)(2,1)S(1)}, u32[]{:S(2)}, u32[]{:S(2)}) collective-permute-start(bf16[2,1,1,256]{3,2,1,0:T(2,128)(2,1)S(1)} %get-tuple-element.80), channel_id=1, source_target_pairs={{0,1},{1,2},{2,3},{4,5},{5,6},{6,7},{8,9},{9,10},{10,11},{12,13},{... | collective-permute-start | bytes 3080 | tf_op jit(solution)/shard_map/ppermute | solution.py:34
  300.6 12.9 %collective-permute-start.18 = (bf16[2,1,1,256]{3,2,1,0:T(2,128)(2,1)S(1)}, bf16[2,1,1,256]{3,2,1,0:T(2,128)(2,1)S(1)}, u32[]{:S(2)}, u32[]{:S(2)}) collective-permute-start(bf16[2,1,1,256]{3,2,1,0:T(2,128)(2,1)S(1)} %get-tuple-element.81), channel_id=1, source_target_pairs={{1,0},{2,1},{3,2},{5,4},{6,5},{7,6},{9,8},{10,9},{11,10},{13,12},{... | collective-permute-start | bytes 3080 | tf_op jit(solution)/shard_map/ppermute | solution.py:37
  370.1 11.7 %collective-permute-start.27 = (bf16[2,1,32,256]{3,2,1,0:T(8,128)(2,1)S(1)}, bf16[2,1,32,256]{3,2,1,0:T(8,128)(2,1)S(1)}, u32[]{:S(2)}, u32[]{:S(2)}) collective-permute-start(bf16[2,1,32,256]{3,2,1,0:T(8,128)(2,1)S(1)} %get-tuple-element.34), channel_id=1, source_target_pairs={{4,0},{8,4},{12,8},{16,12},{20,16},{24,20},{28,24},{32,28},{36,32}... | collective-permute-start | bytes 98312 | tf_op jit(solution)/shard_map/ppermute | solution.py:26
  371.4 11.7 %collective-permute-start.28 = (bf16[2,1,32,256]{3,2,1,0:T(8,128)(2,1)S(1)}, bf16[2,1,32,256]{3,2,1,0:T(8,128)(2,1)S(1)}, u32[]{:S(2)}, u32[]{:S(2)}) collective-permute-start(bf16[2,1,32,256]{3,2,1,0:T(8,128)(2,1)S(1)} %get-tuple-element.34), channel_id=1, source_target_pairs={{0,4},{4,8},{8,12},{12,16},{16,20},{20,24},{24,28},{28,32},{32,36}... | collective-permute-start | bytes 98312 | tf_op jit(solution)/shard_map/ppermute | solution.py:26
  375.6 17.1 %collective-permute-start.25 = (bf16[2,1,1,256]{3,2,1,0:T(2,128)(2,1)S(1)}, bf16[2,1,1,256]{3,2,1,0:T(2,128)(2,1)S(1)}, u32[]{:S(2)}, u32[]{:S(2)}) collective-permute-start(bf16[2,1,1,256]{3,2,1,0:T(2,128)(2,1)S(1)} %get-tuple-element.78), channel_id=1, source_target_pairs={{0,1},{1,2},{2,3},{4,5},{5,6},{6,7},{8,9},{9,10},{10,11},{12,13},{... | collective-permute-start | bytes 3080 | tf_op jit(solution)/shard_map/ppermute | solution.py:34
  379.8 12.9 %collective-permute-start.26 = (bf16[2,1,1,256]{3,2,1,0:T(2,128)(2,1)S(1)}, bf16[2,1,1,256]{3,2,1,0:T(2,128)(2,1)S(1)}, u32[]{:S(2)}, u32[]{:S(2)}) collective-permute-start(bf16[2,1,1,256]{3,2,1,0:T(2,128)(2,1)S(1)} %get-tuple-element.79), channel_id=1, source_target_pairs={{1,0},{2,1},{3,2},{5,4},{6,5},{7,6},{9,8},{10,9},{11,10},{13,12},{... | collective-permute-start | bytes 3080 | tf_op jit(solution)/shard_map/ppermute | solution.py:37
  452.4 11.7 %collective-permute-start.35 = (bf16[2,1,32,256]{3,2,1,0:T(8,128)(2,1)S(1)}, bf16[2,1,32,256]{3,2,1,0:T(8,128)(2,1)S(1)}, u32[]{:S(2)}, u32[]{:S(2)}) collective-permute-start(bf16[2,1,32,256]{3,2,1,0:T(8,128)(2,1)S(1)} %get-tuple-element.30), channel_id=1, source_target_pairs={{4,0},{8,4},{12,8},{16,12},{20,16},{24,20},{28,24},{32,28},{36,32}... | collective-permute-start | bytes 98312 | tf_op jit(solution)/shard_map/ppermute | solution.py:26
  453.7 11.7 %collective-permute-start.36 = (bf16[2,1,32,256]{3,2,1,0:T(8,128)(2,1)S(1)}, bf16[2,1,32,256]{3,2,1,0:T(8,128)(2,1)S(1)}, u32[]{:S(2)}, u32[]{:S(2)}) collective-permute-start(bf16[2,1,32,256]{3,2,1,0:T(8,128)(2,1)S(1)} %get-tuple-element.30), channel_id=1, source_target_pairs={{0,4},{4,8},{8,12},{12,16},{16,20},{20,24},{24,28},{28,32},{32,36}... | collective-permute-start | bytes 98312 | tf_op jit(solution)/shard_map/ppermute | solution.py:26
  458.0 17.1 %collective-permute-start.33 = (bf16[2,1,1,256]{3,2,1,0:T(2,128)(2,1)S(1)}, bf16[2,1,1,256]{3,2,1,0:T(2,128)(2,1)S(1)}, u32[]{:S(2)}, u32[]{:S(2)}) collective-permute-start(bf16[2,1,1,256]{3,2,1,0:T(2,128)(2,1)S(1)} %get-tuple-element.76), channel_id=1, source_target_pairs={{0,1},{1,2},{2,3},{4,5},{5,6},{6,7},{8,9},{9,10},{10,11},{12,13},{... | collective-permute-start | bytes 3080 | tf_op jit(solution)/shard_map/ppermute | solution.py:34
  462.2 12.9 %collective-permute-start.34 = (bf16[2,1,1,256]{3,2,1,0:T(2,128)(2,1)S(1)}, bf16[2,1,1,256]{3,2,1,0:T(2,128)(2,1)S(1)}, u32[]{:S(2)}, u32[]{:S(2)}) collective-permute-start(bf16[2,1,1,256]{3,2,1,0:T(2,128)(2,1)S(1)} %get-tuple-element.77), channel_id=1, source_target_pairs={{1,0},{2,1},{3,2},{5,4},{6,5},{7,6},{9,8},{10,9},{11,10},{13,12},{... | collective-permute-start | bytes 3080 | tf_op jit(solution)/shard_map/ppermute | solution.py:37
  (40 other events, 705.7 us)
where the time goes:
time: 550 us; the launch traced here: 544 us
  blocking collectives  220 us (40%)
  starting transfers between devices  176 us (32%)
  matrix products  70.1 us (13%)
  waiting for transfers between devices  41 us (7%)
  local copies, waits for them, and re-layouts  17.8 us (3%)
  other arithmetic  13.5 us (2%)
    psum x20, blocking collectives, over_axes(): array = lax.psum(array, axis)  220 us
    ppermute x33, starting transfers between devices, from_behind(): return lax.ppermute(array, axis, pairs)  128 us
    dot_general x22, matrix products, left_product(): jnp.einsum('ja,pak->pjk', table, right, preferred_element_type=jnp.float32)  40.7 us
    ppermute x4, starting transfers between devices, extended(): lax.ppermute(lax.slice_in_dim(block, block.shape[dim] - width, None, axis...  40 us
    ppermute x33, waiting for transfers between devices, from_behind(): return lax.ppermute(array, axis, pairs)  38.2 us
    dot_general x14, matrix products, right_product(): jnp.einsum('pab,bk->pak', left, table, preferred_element_type=jnp.float32)  23.9 us
  transfers between devices with their start and end apart: 41, of which 8 were waited for; matrix products, arithmetic and copies ran while one was open for 16% of the time, Pallas kernels for 0%

commit v1 on v0

v1 whole, which is shorter than its diff:
```python
import functools

import numpy as np

import jax
import jax.numpy as jnp
from jax import lax
from jax.experimental import pallas as pl
from jax.experimental.pallas import tpu as pltpu
from jax.sharding import PartitionSpec as P

SUB = 16
ITERS = 4
LINE = 4
CHUNKS = 16

lattice_stiff = 0.5
clip_level = 5.0
step_size = 0.2
floor_ratio = 0.4
tiny_eps = 1e-06

MESH = pl.DeviceIdType.MESH
F32 = jnp.float32
BF16 = jnp.bfloat16
PAIRS = [(i, j) for i in range(ITERS) for j in range(i, ITERS)]


def tables(length):
    series = np.arange(length)
    angles = 2.0 * np.pi / length * (series[:, None] * series[None, :] % length)
    cosine = np.cos(angles).astype(jnp.bfloat16)
    sine = np.sin(angles).astype(jnp.bfloat16)
    right = np.concatenate([cosine, sine], axis=1)
    left = np.block([[cosine, -sine], [-sine, -cosine]])
    back = np.block([[cosine, sine], [-sine, cosine]])
    last = np.concatenate([cosine, -sine], axis=1)
    return right, left, back, last


def kernel(
    depth,
    tiles,
    patches,
    offsets,
    offsets_v,
    masks,
    start,
    right,
    left,
    back,
    last,
    positions,
    targets,
    surfaces,
    norms,
    own,
    near,
    cross,
    spec_real,
    spec_imag,
    staged,
    taps,
    send_z,
    recv_z,
    send_e,
    recv_e,
    weight_t,
    weight_l,
    target_t,
    target_l,
    weights,
    fields,
    gram,
    gram_a,
    gram_b,
    local_sem,
    surf_sem,
    ps,
    pr,
    zs,
    zr,
    es,
    er,
    ws,
    wr,
    ts,
    tr,
    gs,
    gr,
):
    z = lax.axis_index("gz")
    t = lax.axis_index("xy")
    count, length, _ = own.shape
    piece = count // CHUNKS
    columns = masks.shape[2]
    rows_dev = masks.shape[1]
    lines = depth // LINE
    y = lax.rem(z, LINE)
    line = lax.div(z, LINE)
    has_next = line < lines - 1
    has_prev = line > 0
    group = LINE * tiles
    me = y * tiles + t

    def remote(src, dst, send, recv, gz, xy):
        return pltpu.make_async_remote_copy(
            src_ref=src, dst_ref=dst, send_sem=send, recv_sem=recv, device_id=(gz, xy), device_id_type=MESH
        )

    def local_copy(c):
        part = pl.ds(c * piece, piece)
        return pltpu.make_async_copy(patches.at[part], own.at[part], local_sem.at[c])

    def start_local(c, carry):
        local_copy(c).start()
        return carry

    lax.fori_loop(0, CHUNKS, start_local, 0)

    barrier = pltpu.get_barrier_semaphore()

    def greet_group(i, carry):
        other = lax.rem(me + i, group)
        gz = line * LINE + lax.div(other, tiles)
        pl.semaphore_signal(barrier, inc=1, device_id=(gz, lax.rem(other, tiles)), device_id_type=MESH)
        return carry

    lax.fori_loop(1, group, greet_group, 0)

    def greet_lines(i, carry):
        other = lax.rem(line + i, lines)
        pl.semaphore_signal(barrier, inc=1, device_id=(other * LINE + y, t), device_id_type=MESH)
        return carry

    lax.fori_loop(1, lines, greet_lines, 0)
    for k in range(1, 4):
        for sign in (-1, 1):
            there = z + sign * k

            @pl.when((there >= 0) & (there < depth))
            def _():
                pl.semaphore_signal(barrier, inc=1, device_id=(there, t), device_id_type=MESH)

    for k in range(1, 4):

        @pl.when(z + k >= depth)
        def _():
            near[k - 1] = jnp.zeros(near.shape[1:], BF16)
            for r in range(ITERS):
                recv_z[r, k - 1] = jnp.zeros(recv_z.shape[2:], BF16)

        @pl.when(z - k < 0)
        def _():
            for r in range(ITERS):
                recv_z[r, 2 + k] = jnp.zeros(recv_z.shape[2:], BF16)
            weight_l[k - 1] = jnp.zeros(weight_l.shape[1:], F32)
            target_l[k - 1] = jnp.zeros(target_l.shape[1:], F32)

    weight_t[...] = jnp.zeros(weight_t.shape, F32)
    target_t[...] = jnp.zeros(target_t.shape, F32)
    taps[...] = jnp.zeros(taps.shape, F32)
    for k in range(1, 4):
        live = jnp.where(z + k < depth, 1.0 / k, 0.0).astype(F32)
        weight_t[2 * (k - 1) : 2 * k, 0:columns] = masks[k - 1].astype(F32) * live

    def stage(r, value):
        for a in range(2):
            send_z[r, a] = value[a].astype(BF16)
            send_e[r, 0, a : a + 1] = value[a][0:1]
            send_e[r, 1, a : a + 1] = value[a][-1:]

    start_value = [start[0], start[1]]
    stage(0, start_value)

    expected = group - 1 + lines - 1
    for k in range(1, 4):
        expected = expected + (z + k < depth).astype(jnp.int32) + (z - k >= 0).astype(jnp.int32)
    pl.semaphore_wait(barrier, expected)

    def z_copy(r, k, sign):
        slot = 2 + k if sign > 0 else k - 1
        return remote(send_z.at[r], recv_z.at[r, slot], zs.at[r, slot], zr.at[r, slot], z + sign * k, t)

    def e_copy(r, sign):
        side = 1 if sign > 0 else 0
        return remote(send_e.at[r, side], recv_e.at[r, 1 - side], es.at[r, side], er.at[r, 1 - side], z, t + sign)

    def exchange_start(r):
        for k in (3, 2, 1):
            for sign in (-1, 1):

                @pl.when((z + sign * k >= 0) & (z + sign * k < depth))
                def _():
                    z_copy(r, k, sign).start()

        for sign in (-1, 1):

            @pl.when((t + sign >= 0) & (t + sign < tiles))
            def _():
                e_copy(r, sign).start()

    def exchange_wait(r):
        for k in (1, 2, 3):
            for sign in (-1, 1):

                @pl.when((z - sign * k >= 0) & (z - sign * k < depth))
                def _():
                    z_copy(r, k, sign).wait_recv()

        for sign in (-1, 1):

            @pl.when((t - sign >= 0) & (t - sign < tiles))
            def _():
                e_copy(r, sign).wait_recv()

    def exchange_drain(r):
        for k in (1, 2, 3):
            for sign in (-1, 1):

                @pl.when((z + sign * k >= 0) & (z + sign * k < depth))
                def _():
                    z_copy(r, k, sign).wait_send()

        for sign in (-1, 1):

            @pl.when((t + sign >= 0) & (t + sign < tiles))
            def _():
                e_copy(r, sign).wait_send()

    def w_copy(k):
        return remote(weight_t, weight_l.at[k - 1], ws.at[k - 1], wr.at[k - 1], z + k, t)

    def t_copy(k):
        return remote(target_t.at[k - 1], target_l.at[k - 1], ts.at[k - 1], tr.at[k - 1], z + k, t)

    def part_of(c):
        return pl.ds(c * piece, piece)

    def patch_copy(src, dst, send, slot, c, gz):
        part = part_of(c)
        return remote(src.at[part], dst.at[part], ps.at[send], pr.at[slot, c], gz, t)

    own_sends = [
        ((y < LINE - 1) & has_prev, own, cross, 0, 3, z - LINE),
        (y >= 1, own, near.at[0], 1, 0, z - 1),
        (y == LINE - 1, own, near.at[2], 2, 2, z - 3),
    ]
    cross_sends = [
        ((y < LINE - 1) & has_next, cross, near.at[2], 3, 2, z + 1),
        ((y == 0) & has_next, cross, near.at[0], 4, 0, z + 3),
    ]
    first_sends = [((y == 1) | (y == 2), near.at[0], near.at[1], 5, 1, z - 1)]
    third_sends = [(((y == 1) | (y == 2)) & has_next, near.at[2], near.at[1], 6, 1, z + 1)]
    all_sends = own_sends + cross_sends + first_sends + third_sends

    def send_all(sends, c):
        for condition, src, dst, send, slot, gz in sends:

            @pl.when(condition)
            def _():
                patch_copy(src, dst, send, slot, c, gz).start()

    def arrived(slot, c):
        buffer = cross if slot == 3 else near.at[slot]
        patch_copy(buffer, buffer, 0, slot, c, z).wait_recv()

    exchange_start(0)
    for k in range(1, 4):

        @pl.when(z + k < depth)
        def _():
            w_copy(k).start()

    def send_own(c, carry):
        local_copy(c).wait()
        send_all(own_sends, c)
        return carry

    lax.fori_loop(0, CHUNKS, send_own, 0)

    half = length

    def dot(a, b):
        return jnp.dot(a, b, preferred_element_type=F32)

    def side_by_side(m):
        return jnp.concatenate(
            [
                jnp.concatenate([m[:half, :half], m[half:, :half]], axis=1),
                jnp.concatenate([m[:half, half:], m[half:, half:]], axis=1),
            ],
            axis=0,
        )

    def spectra(ref, p):
        pair = ref[pl.ds(p, 2)].reshape(2 * half, half)
        mixed = dot(pair, right[...]).astype(BF16)
        return dot(left[...], side_by_side(mixed))

    def own_spectra(c):
        def body(i, carry):
            p = c * piece + 2 * i
            s = spectra(own, p)
            for a in range(2):
                cols = slice(a * half, (a + 1) * half)
                spec_real[p + a] = s[:half, cols]
                spec_imag[p + a] = s[half:, cols]
            return carry

        lax.fori_loop(0, piece // 2, body, 0)

    row_id = lax.broadcasted_iota(jnp.int32, (16, length), 0)
    row_id = jnp.where(row_id < 8, row_id, row_id - 16)
    col_id = lax.broadcasted_iota(jnp.int32, (16, length), 1)
    col_id = jnp.where(col_id < length // 2, col_id, col_id - length)
    tap_row = lax.broadcasted_iota(jnp.int32, (8, length), 0)
    tap_col = lax.broadcasted_iota(jnp.int32, (8, length), 1)

    def pick(k, p, window):
        r = lax.div(p, columns)
        c = lax.rem(p, columns)
        d_row = row_id - offsets[2 * k, r, c]
        d_col = col_id - offsets[2 * k + 1, r, c]
        down = jnp.where((d_col == 0) & (jnp.abs(d_row) <= 1), window, 0.0)
        across = jnp.where((d_row == 0) & (jnp.abs(d_col) <= 1), window, 0.0)

        def total(v):
            return jnp.sum(jnp.sum(v, axis=0, keepdims=True), axis=1, keepdims=True)

        sums = (
            total(down * d_row.astype(F32)),
            total(jnp.abs(down)),
            total(across * d_col.astype(F32)),
            total(jnp.abs(across)),
        )
        value = taps[k]
        for q in range(4):
            value = jnp.where((tap_row == 2 * q + r) & (tap_col == c), sums[q], value)
        taps[k] = value

    def correlate(k, c):
        def body(i, carry):
            p = c * piece + 2 * i
            s = spectra(near.at[k], p)
            mixed = []
            for a in range(2):
                cols = slice(a * half, (a + 1) * half)
                b_real, b_imag = s[:half, cols], s[half:, cols]
                a_real, a_imag = spec_real[p + a], spec_imag[p + a]
                real = (a_real * b_real + a_imag * b_imag).astype(BF16)
                imag = (a_real * b_imag - a_imag * b_real).astype(BF16)
                mixed.append(jnp.concatenate([real, imag], axis=1))
            halves = dot(jnp.concatenate(mixed, axis=0), back[...]).astype(BF16)
            corr = dot(last[...], side_by_side(halves)) * (1.0 / (length * length))
            for a in range(2):
                one = corr[:, a * half : (a + 1) * half]
                staged[k, p + a] = one.astype(BF16)
                pick(k, p + a, jnp.concatenate([one[:8], one[length - 8 :]], axis=0))
            return carry

        lax.fori_loop(0, piece // 2, body, 0)
        part = part_of(c)
        pltpu.make_async_copy(staged.at[k, part], surfaces.at[k, part], surf_sem).start()

    def step(c, carry):
        @pl.when(c < CHUNKS)
        def _():
            own_spectra(c)

            @pl.when(z + 1 < depth)
            def _():
                arrived(0, c)

            send_all(first_sends, c)

            @pl.when((y < LINE - 1) & has_next)
            def _():
                arrived(3, c)

            send_all(cross_sends, c)
            correlate(0, c)

        @pl.when((c >= 1) & (c < CHUNKS + 1))
        def _():
            @pl.when(z + 3 < depth)
            def _():
                arrived(2, c - 1)

            send_all(third_sends, c - 1)
            correlate(2, c - 1)

        @pl.when(c >= 2)
        def _():
            @pl.when(z + 2 < depth)
            def _():
                arrived(1, c - 2)

            correlate(1, c - 2)

        return carry

    lax.fori_loop(0, CHUNKS + 2, step, 0)

    for k in range(1, 4):
        sums = taps[k - 1]
        weight = weight_t[2 * (k - 1) : 2 * k, 0:columns]
        for a in range(2):
            slope = sums[4 * a : 4 * a + 2, 0:columns]
            size = sums[4 * a + 2 : 4 * a + 4, 0:columns]
            shift = offsets_v[2 * (k - 1) + a].astype(F32)
            value = shift + slope / jnp.maximum(size, floor_ratio * length)
            targets[2 * (k - 1) + a] = value
            target_t[k - 1, 2 * a : 2 * a + 2, 0:columns] = weight * value
    for k in range(1, 4):

        @pl.when(z + k < depth)
        def _():
            t_copy(k).start()

    nodes_rows, nodes_cols = start.shape[1], start.shape[2]
    spread = (
        lax.broadcasted_iota(jnp.int32, (length, nodes_cols), 0)
        == lax.shift_right_logical(lax.broadcasted_iota(jnp.int32, (length, nodes_cols), 1), 4)
    ).astype(F32)

    def widen(small):
        return jnp.dot(small, spread, precision=lax.Precision.HIGHEST, preferred_element_type=F32)

    def tall(wide, first):
        return jnp.concatenate(
            [jnp.broadcast_to(wide[first + r : first + r + 1], (SUB, nodes_cols)) for r in range(rows_dev)], axis=0
        )

    wide_own = widen(weight_t[...])
    for k in range(1, 4):

        @pl.when(z - k >= 0)
        def _():
            w_copy(k).wait_recv()

        weights[k - 1] = tall(wide_own, 2 * (k - 1))
        weights[2 + k] = tall(widen(weight_l[k - 1]), 2 * (k - 1))

    node_row = lax.broadcasted_iota(jnp.int32, (nodes_rows, nodes_cols), 0)
    node_col = lax.broadcasted_iota(jnp.int32, (nodes_rows, nodes_cols), 1)

    def linear(r, value):
        result = []
        for a in range(2):
            u = value[a]
            upper = jnp.where(t == 0, u[0:1], recv_e[r, 0, a : a + 1])
            lower = jnp.where(t == tiles - 1, u[-1:], recv_e[r, 1, a : a + 1])
            up = jnp.where(node_row == 0, upper, pltpu.roll(u, 1, 0))
            down = jnp.where(node_row == nodes_rows - 1, lower, pltpu.roll(u, nodes_rows - 1, 0))
            west = jnp.where(node_col == 0, u, pltpu.roll(u, 1, 1))
            east = jnp.where(node_col == nodes_cols - 1, u, pltpu.roll(u, nodes_cols - 1, 1))
            force = lattice_stiff * (up + down + west + east - 4.0 * u)
            for k in range(1, 4):
                force = force + weights[k - 1] * (recv_z[r, k - 1, a].astype(F32) - u)
                force = force - weights[2 + k] * (u - recv_z[r, 2 + k, a].astype(F32))
            result.append(force)
        return result

    exchange_wait(0)
    base = linear(0, start_value)

    for k in range(1, 4):

        @pl.when(z - k >= 0)
        def _():
            t_copy(k).wait_recv()

    pull = target_l[0] + target_l[1] + target_l[2] - target_t[0] - target_t[1] - target_t[2]
    wide_pull = widen(pull)
    value = [base[a] + tall(wide_pull, 2 * a) for a in range(2)]
    for i in range(ITERS):
        for a in range(2):
            fields[i, a] = value[a]
        if i < ITERS - 1:
            stage(i + 1, value)
            exchange_start(i + 1)
        for n, (first, second) in enumerate(PAIRS):
            if second == i:
                product = fields[first, 0] * value[0] + fields[first, 1] * value[1]
                row = jnp.sum(product, axis=0, keepdims=True)
                gram[n : n + 1] = row[:, :length] + row[:, length:]
        if i < ITERS - 1:
            exchange_wait(i + 1)
            moved = linear(i + 1, value)
            value = [value[a] + step_size * moved[a] for a in range(2)]

    def group_copy(i):
        other = lax.rem(me + i, group)
        return remote(
            gram, gram_a.at[me], gs.at[0, i], gr.at[0, i], line * LINE + lax.div(other, tiles), lax.rem(other, tiles)
        )

    def lines_copy(i):
        other = lax.rem(line + i, lines)
        return remote(gram, gram_b.at[line], gs.at[1, i], gr.at[1, i], other * LINE + y, t)

    def run(copy, number, what):
        def body(i, carry):
            getattr(copy(i), what)()
            return carry

        lax.fori_loop(1, number, body, 0)

    for n in range(len(PAIRS), gram.shape[0]):
        gram[n : n + 1] = jnp.zeros((1, length), F32)
    run(group_copy, group, "start")
    gram_a[me] = gram[...]
    run(group_copy, group, "wait")
    total = gram_a[0]
    for i in range(1, group):
        total = total + gram_a[i]
    gram[...] = total
    run(lines_copy, lines, "start")
    gram_b[line] = total
    run(lines_copy, lines, "wait")
    total = gram_b[0]
    for i in range(1, lines):
        total = total + gram_b[i]
    total = jnp.broadcast_to(jnp.sum(total, axis=1, keepdims=True), total.shape)

    entries = {}
    for n, (first, second) in enumerate(PAIRS):
        entries[first, second] = entries[second, first] = total[n : n + 1]
    number = 2.0 * depth * tiles * nodes_rows * nodes_cols
    ones = jnp.ones((1, length), F32)
    coefficients = [ones]
    sums = [jnp.zeros((1, length), F32)] * ITERS
    for i in range(ITERS):
        square = jnp.zeros((1, length), F32)
        for first in range(len(coefficients)):
            for second in range(len(coefficients)):
                square = square + coefficients[first] * coefficients[second] * entries[first, second]
        rms = jnp.sqrt(jnp.maximum(square, 0.0) / number + tiny_eps)
        norms[i : i + 1] = rms
        factor = jnp.minimum(1.0, clip_level / rms)
        for n in range(len(coefficients)):
            sums[n] = sums[n] + step_size * factor * coefficients[n]
        kept = [(1.0 - factor) * value for value in coefficients] + [0.0 * ones]
        shifted = [0.0 * ones] + [factor * value for value in coefficients]
        coefficients = [kept[n] + shifted[n] for n in range(len(shifted))]
    for a in range(2):
        result = start[a]
        for n in range(ITERS):
            result = result + jnp.concatenate([sums[n], sums[n]], axis=1) * fields[n, a]
        positions[a] = result

    for k in range(1, 4):

        @pl.when(z + k < depth)
        def _():
            w_copy(k).wait_send()
            t_copy(k).wait_send()

    for r in range(ITERS):
        exchange_drain(r)
    for condition, src, dst, send, slot, gz in all_sends:

        @pl.when(condition)
        def _():
            remote(src, dst, ps.at[send], pr.at[slot, 0], gz, t).wait_send()

    pltpu.make_async_copy(staged, surfaces, surf_sem).wait()


def local(depth, tiles, patches, peak_offsets, valid_masks, initial_positions):
    _, rows_dev, columns, length, _ = patches.shape
    count = rows_dev * columns
    _, _, nodes_rows, nodes_cols = initial_positions.shape
    offsets = peak_offsets.reshape(6, rows_dev, columns)
    vmem = pl.BlockSpec(memory_space=pltpu.VMEM)
    smem = pl.BlockSpec(memory_space=pltpu.SMEM)
    hbm = pl.BlockSpec(memory_space=pl.ANY)
    group = LINE * tiles
    lines = depth // LINE
    dma = pltpu.SemaphoreType.DMA
    flops = 2 * count * (4 * 6 + 3 * 6) * length**3
    outs = pl.pallas_call(
        functools.partial(kernel, depth, tiles),
        out_shape=(
            jax.ShapeDtypeStruct((2, nodes_rows, nodes_cols), F32),
            jax.ShapeDtypeStruct((6, rows_dev, columns), F32),
            jax.ShapeDtypeStruct((3, count, length, length), BF16),
            jax.ShapeDtypeStruct((ITERS, length), F32),
        ),
        in_specs=[hbm, smem, vmem, vmem, vmem, vmem, vmem, vmem, vmem],
        out_specs=(vmem, vmem, hbm, vmem),
        scratch_shapes=[
            pltpu.VMEM((count, length, length), BF16),
            pltpu.VMEM((3, count, length, length), BF16),
            pltpu.VMEM((count, length, length), BF16),
            pltpu.VMEM((count, length, length), F32),
            pltpu.VMEM((count, length, length), F32),
            pltpu.VMEM((3, count, length, length), BF16),
            pltpu.VMEM((3, 8, length), F32),
            pltpu.VMEM((ITERS, 2, nodes_rows, nodes_cols), BF16),
            pltpu.VMEM((ITERS, 6, 2, nodes_rows, nodes_cols), BF16),
            pltpu.VMEM((ITERS, 2, 8, nodes_cols), F32),
            pltpu.VMEM((ITERS, 2, 8, nodes_cols), F32),
            pltpu.VMEM((8, length), F32),
            pltpu.VMEM((3, 8, length), F32),
            pltpu.VMEM((3, 8, length), F32),
            pltpu.VMEM((3, 8, length), F32),
            pltpu.VMEM((6, nodes_rows, nodes_cols), F32),
            pltpu.VMEM((ITERS, 2, nodes_rows, nodes_cols), F32),
            pltpu.VMEM((16, length), F32),
            pltpu.VMEM((group, 16, length), F32),
            pltpu.VMEM((lines, 16, length), F32),
            dma((CHUNKS,)),
            dma,
            dma((7,)),
            dma((4, CHUNKS)),
            dma((ITERS, 6)),
            dma((ITERS, 6)),
            dma((ITERS, 2)),
            dma((ITERS, 2)),
            dma((3,)),
            dma((3,)),
            dma((3,)),
            dma((3,)),
            dma((2, max(group, lines))),
            dma((2, max(group, lines))),
        ],
        compiler_params=pltpu.CompilerParams(collective_id=0, has_side_effects=True),
        cost_estimate=pl.CostEstimate(flops=flops, bytes_accessed=5 * count * length * length * 2, transcendentals=0),
    )(
        patches.reshape(count, length, length),
        offsets,
        offsets,
        valid_masks.reshape(3, rows_dev, columns),
        initial_positions.reshape(2, nodes_rows, nodes_cols),
        *[jnp.asarray(table) for table in tables(length)],
    )
    positions, targets, surfaces, norms = outs
    return (
        positions.reshape(initial_positions.shape),
        targets.reshape(peak_offsets.shape),
        surfaces.reshape(1, 3, rows_dev, columns, length, length),
        norms[:, 0],
    )


def solution(mesh):
    depth, tiles = mesh.shape["gz"], mesh.shape["xy"]
    placed = (
        P("gz", "xy", None, None, None),
        P("gz", None, "xy", None),
        P("gz", None, "xy", None),
        P(None, "gz", "xy", None),
    )
    return jax.shard_map(
        functools.partial(local, depth, tiles),
        mesh=mesh,
        in_specs=placed,
        out_specs=(
            P(None, "gz", "xy", None),
            P("gz", None, "xy", None),
            P("gz", None, "xy", None, None, None),
            P(),
        ),
        check_vma=False,
    )
```

time: 550 us -> 137 us (0.25); the launches traced: 544 us -> 137 us
  blocking collectives: 220 us -> 0 us
  starting transfers between devices: 176 us -> 0 us
  Pallas kernels: 0 us -> 128 us
  matrix products: 70.1 us -> 0 us
  waiting for transfers between devices: 41 us -> 0 us
  other arithmetic: 13.5 us -> 0 us
  local copies, waits for them, and re-layouts: 17.8 us -> 8.01 us
    psum x20 -> x0, blocking collectives: 220 us -> none  [over_axes(): array = lax.psum(array, axis)]
    ppermute x41 -> x0, starting transfers between devices: 176 us -> none  [the longest x33 128 us: from_behind(): return lax.ppermute(array, axis, pairs)]
    pallas_call x0 -> x1, Pallas kernels: none -> 128 us  [local(): pl.pallas_call(functools.partial(kernel, depth, tiles), out_shape=(jax.Sh...]
    dot_general x39 -> x0, matrix products: 70.1 us -> none  [the longest x22 40.7 us: left_product(): jnp.einsum('ja,pak->pjk', table, right, preferred_element_type=jnp.float32)]
    ppermute x41 -> x0, waiting for transfers between devices: 41 us -> none  [the longest x33 38.2 us: from_behind(): return lax.ppermute(array, axis, pairs)]
  transfers between devices with their start and end apart: 41 -> 0, of which waited for: 8 -> 0; matrix products, arithmetic and copies ran while one was open for 16% -> 0% of each run, Pallas kernels for 0% -> 0%
where the time goes in v1:
time: 137 us
  Pallas kernels  128 us (93%)
  local copies, waits for them, and re-layouts  8.01 us (6%)
    pallas_call x1, Pallas kernels, local(): pl.pallas_call(functools.partial(kernel, depth, tiles), out_shape=(jax.Sh...  128 us
    unnamed x3, local copies, waits for them, and re-layouts  6.72 us

profile of v1, /device:TPU:1, one launch (start us, length us, event | category | flops | bytes accessed | tf_op | source)
XLA Modules:
  0.0 136.8 jit_solution(13711508027974265360)
XLA Ops:
  0.6 128.2 %shard_map.111 = (f32[2,32,256]{2,1,0:T(8,128)}, f32[6,2,16]{2,1,0:T(2,128)}, bf16[3,32,128,128]{3,2,1,0:T(8,128)(2,1)}, f32[4,128]{1,0:T(4,128)}) custom-call(bf16[32,128,128]{2,1,0:T(8,128)(2,1)} %bitcast.12, s32[6,2,16]{2,1,0:T(2,128)} %bitcast.14, s32[6,2,16]{2,1,0:T(2,128)} %bitcast.15, s32[3,2,16]{2,1,0:T(2,128)} %bitcast.16, f32[2,32,256]{2,1,0:T(8,128)} %bitcast.13, ...), custom_call_target="tpu_custom_call" | custom-call | flops 5637144576 | bytes 5242880 | tf_op jit(solution)/shard_map/pallas_call | solution.py:583
  128.8 1.3 slice_reduce_fusion
  130.1 1.5 %copy.17 = f32[2,1,32,256]{3,2,1,0:T(8,128)} copy(f32[2,1,32,256]{3,2,1,0:T(8,128)} %bitcast.10) | data formatting | bytes 131072
  131.6 1.3 copy.18
  132.9 4.0 %copy.19 = bf16[1,3,2,16,128,128]{5,4,3,2,1,0:T(8,128)(2,1)} copy(bf16[1,3,2,16,128,128]{5,4,3,2,1,0:T(8,128)(2,1)} %bitcast.9) | data formatting | bytes 6291456

commit v2 on v1

--- a/solution.py
+++ b/solution.py
@@ -13,6 +13,9 @@
 ITERS = 4
 LINE = 4
 CHUNKS = 16
+AHEAD = 4
+OWN_STEP = 8
+LAG = 2
 
 lattice_stiff = 0.5
 clip_level = 5.0
@@ -35,31 +38,32 @@
     left = np.block([[cosine, -sine], [-sine, -cosine]])
     back = np.block([[cosine, sine], [-sine, cosine]])
     last = np.concatenate([cosine, -sine], axis=1)
-    return right, left, back, last
+    return np.concatenate([right, left, back, last], axis=0)
 
 
 def kernel(
     depth,
     tiles,
     patches,
+    offsets_h,
+    masks_h,
+    start_h,
+    tables_h,
+    targets,
+    surfaces,
+    fields,
+    gram_out,
+    own,
+    near,
+    passing,
+    spec_real,
+    spec_imag,
+    staged,
     offsets,
     offsets_v,
     masks,
     start,
-    right,
-    left,
-    back,
-    last,
-    positions,
-    targets,
-    surfaces,
-    norms,
-    own,
-    near,
-    cross,
-    spec_real,
-    spec_imag,
-    staged,
+    table,
     taps,
     send_z,
     recv_z,
@@ -70,11 +74,12 @@
     target_t,
     target_l,
     weights,
-    fields,
     gram,
+    gram_row,
     gram_a,
     gram_b,
     local_sem,
+    in_sem,
     surf_sem,
     ps,
     pr,
@@ -93,8 +98,8 @@
     t = lax.axis_index("xy")
     count, length, _ = own.shape
     piece = count // CHUNKS
-    columns = masks.shape[2]
-    rows_dev = masks.shape[1]
+    columns = masks_h.shape[2]
+    rows_dev = masks_h.shape[1]
     lines = depth // LINE
     y = lax.rem(z, LINE)
     line = lax.div(z, LINE)
@@ -112,6 +117,19 @@
         part = pl.ds(c * piece, piece)
         return pltpu.make_async_copy(patches.at[part], own.at[part], local_sem.at[c])
 
+    inputs = [
+        pltpu.make_async_copy(source, held, in_sem.at[n])
+        for n, (source, held) in enumerate(
+            ((masks_h, masks), (start_h, start), (offsets_h, offsets_v), (offsets_h, offsets), (tables_h, table))
+        )
+    ]
+    for copy in inputs:
+        copy.start()
+    right = table.at[0:length]
+    left = table.at[length : 3 * length]
+    back = table.at[3 * length : 5 * length]
+    last = table.at[5 * length : 6 * length]
+
     def start_local(c, carry):
         local_copy(c).start()
         return carry
@@ -157,6 +175,8 @@
             weight_l[k - 1] = jnp.zeros(weight_l.shape[1:], F32)
             target_l[k - 1] = jnp.zeros(target_l.shape[1:], F32)
 
+    inputs[0].wait()
+    inputs[1].wait()
     weight_t[...] = jnp.zeros(weight_t.shape, F32)
     target_t[...] = jnp.zeros(target_t.shape, F32)
     taps[...] = jnp.zeros(taps.shape, F32)
@@ -173,112 +193,8 @@
     start_value = [start[0], start[1]]
     stage(0, start_value)
 
-    expected = group - 1 + lines - 1
-    for k in range(1, 4):
-        expected = expected + (z + k < depth).astype(jnp.int32) + (z - k >= 0).astype(jnp.int32)
-    pl.semaphore_wait(barrier, expected)
-
-    def z_copy(r, k, sign):
-        slot = 2 + k if sign > 0 else k - 1
-        return remote(send_z.at[r], recv_z.at[r, slot], zs.at[r, slot], zr.at[r, slot], z + sign * k, t)
-
-    def e_copy(r, sign):
-        side = 1 if sign > 0 else 0
-        return remote(send_e.at[r, side], recv_e.at[r, 1 - side], es.at[r, side], er.at[r, 1 - side], z, t + sign)
-
-    def exchange_start(r):
-        for k in (3, 2, 1):
-            for sign in (-1, 1):
-
-                @pl.when((z + sign * k >= 0) & (z + sign * k < depth))
-                def _():
-                    z_copy(r, k, sign).start()
-
-        for sign in (-1, 1):
-
-            @pl.when((t + sign >= 0) & (t + sign < tiles))
-            def _():
-                e_copy(r, sign).start()
-
-    def exchange_wait(r):
-        for k in (1, 2, 3):
-            for sign in (-1, 1):
-
-                @pl.when((z - sign * k >= 0) & (z - sign * k < depth))
-                def _():
-                    z_copy(r, k, sign).wait_recv()
-
-        for sign in (-1, 1):
-
-            @pl.when((t - sign >= 0) & (t - sign < tiles))
-            def _():
-                e_copy(r, sign).wait_recv()
-
-    def exchange_drain(r):
-        for k in (1, 2, 3):
-            for sign in (-1, 1):
-
-                @pl.when((z + sign * k >= 0) & (z + sign * k < depth))
-                def _():
-                    z_copy(r, k, sign).wait_send()
-
-        for sign in (-1, 1):
-
-            @pl.when((t + sign >= 0) & (t + sign < tiles))
-            def _():
-                e_copy(r, sign).wait_send()
-
-    def w_copy(k):
-        return remote(weight_t, weight_l.at[k - 1], ws.at[k - 1], wr.at[k - 1], z + k, t)
-
-    def t_copy(k):
-        return remote(target_t.at[k - 1], target_l.at[k - 1], ts.at[k - 1], tr.at[k - 1], z + k, t)
-
-    def part_of(c):
-        return pl.ds(c * piece, piece)
-
-    def patch_copy(src, dst, send, slot, c, gz):
-        part = part_of(c)
-        return remote(src.at[part], dst.at[part], ps.at[send], pr.at[slot, c], gz, t)
-
-    own_sends = [
-        ((y < LINE - 1) & has_prev, own, cross, 0, 3, z - LINE),
-        (y >= 1, own, near.at[0], 1, 0, z - 1),
-        (y == LINE - 1, own, near.at[2], 2, 2, z - 3),
-    ]
-    cross_sends = [
-        ((y < LINE - 1) & has_next, cross, near.at[2], 3, 2, z + 1),
-        ((y == 0) & has_next, cross, near.at[0], 4, 0, z + 3),
-    ]
-    first_sends = [((y == 1) | (y == 2), near.at[0], near.at[1], 5, 1, z - 1)]
-    third_sends = [(((y == 1) | (y == 2)) & has_next, near.at[2], near.at[1], 6, 1, z + 1)]
-    all_sends = own_sends + cross_sends + first_sends + third_sends
-
-    def send_all(sends, c):
-        for condition, src, dst, send, slot, gz in sends:
-
-            @pl.when(condition)
-            def _():
-                patch_copy(src, dst, send, slot, c, gz).start()
-
-    def arrived(slot, c):
-        buffer = cross if slot == 3 else near.at[slot]
-        patch_copy(buffer, buffer, 0, slot, c, z).wait_recv()
-
-    exchange_start(0)
-    for k in range(1, 4):
-
-        @pl.when(z + k < depth)
-        def _():
-            w_copy(k).start()
-
-    def send_own(c, carry):
-        local_copy(c).wait()
-        send_all(own_sends, c)
-        return carry
-
-    lax.fori_loop(0, CHUNKS, send_own, 0)
-
+    for copy in inputs[2:]:
+        copy.wait()
     half = length
 
     def dot(a, b):
@@ -293,22 +209,128 @@
             axis=0,
         )
 
-    def spectra(ref, p):
-        pair = ref[pl.ds(p, 2)].reshape(2 * half, half)
-        mixed = dot(pair, right[...]).astype(BF16)
-        return dot(left[...], side_by_side(mixed))
-
-    def own_spectra(c):
-        def body(i, carry):
-            p = c * piece + 2 * i
-            s = spectra(own, p)
+    def spectra(sources):
+        mixed = [dot(ref[pl.ds(p, 2)].reshape(2 * half, half), right[...]).astype(BF16) for ref, p in sources]
+        return [dot(left[...], side_by_side(m)) for m in mixed]
+
+    def own_spectra(i, carry):
+        firsts = [OWN_STEP * i + 2 * n for n in range(OWN_STEP // 2)]
+        for p, s in zip(firsts, spectra([(own, p) for p in firsts])):
             for a in range(2):
                 cols = slice(a * half, (a + 1) * half)
                 spec_real[p + a] = s[:half, cols]
                 spec_imag[p + a] = s[half:, cols]
-            return carry
-
-        lax.fori_loop(0, piece // 2, body, 0)
+        return carry
+
+    def wait_local(c, carry):
+        local_copy(c).wait()
+        return carry
+
+    lax.fori_loop(0, CHUNKS, wait_local, 0)
+    lax.fori_loop(0, count // OWN_STEP, own_spectra, 0)
+
+    expected = group - 1 + lines - 1
+    for k in range(1, 4):
+        expected = expected + (z + k < depth).astype(jnp.int32) + (z - k >= 0).astype(jnp.int32)
+    pl.semaphore_wait(barrier, expected)
+
+    def z_copy(r, k, sign):
+        slot = 2 + k if sign > 0 else k - 1
+        return remote(send_z.at[r], recv_z.at[r, slot], zs.at[r, slot], zr.at[r, slot], z + sign * k, t)
+
+    def e_copy(r, sign):
+        side = 1 if sign > 0 else 0
+        return remote(send_e.at[r, side], recv_e.at[r, 1 - side], es.at[r, side], er.at[r, 1 - side], z, t + sign)
+
+    def exchange_start(r):
+        for k in (3, 2, 1):
+            for sign in (-1, 1):
+
+                @pl.when((z + sign * k >= 0) & (z + sign * k < depth))
+                def _():
+                    z_copy(r, k, sign).start()
+
+        for sign in (-1, 1):
+
+            @pl.when((t + sign >= 0) & (t + sign < tiles))
+            def _():
+                e_copy(r, sign).start()
+
+    def exchange_wait(r):
+        for k in (1, 2, 3):
+            for sign in (-1, 1):
+
+                @pl.when((z - sign * k >= 0) & (z - sign * k < depth))
+                def _():
+                    z_copy(r, k, sign).wait_recv()
+
+        for sign in (-1, 1):
+
+            @pl.when((t - sign >= 0) & (t - sign < tiles))
+            def _():
+                e_copy(r, sign).wait_recv()
+
+    def exchange_drain(r):
+        for k in (1, 2, 3):
+            for sign in (-1, 1):
+
+                @pl.when((z + sign * k >= 0) & (z + sign * k < depth))
+                def _():
+                    z_copy(r, k, sign).wait_send()
+
+        for sign in (-1, 1):
+
+            @pl.when((t + sign >= 0) & (t + sign < tiles))
+            def _():
+                e_copy(r, sign).wait_send()
+
+    def w_copy(k):
+        return remote(weight_t, weight_l.at[k - 1], ws.at[k - 1], wr.at[k - 1], z + k, t)
+
+    def t_copy(k):
+        return remote(target_t.at[k - 1], target_l.at[k - 1], ts.at[k - 1], tr.at[k - 1], z + k, t)
+
+    def part_of(c):
+        return pl.ds(c * piece, piece)
+
+    def patch_copy(src, dst, send, slot, c, gz):
+        part = part_of(c)
+        return remote(src.at[part], dst.at[part], ps.at[send], pr.at[slot, c], gz, t)
+
+    relays = (y == 1) | (y == 2)
+    own_sends = [
+        (z >= 3, own, near.at[2], 0, 2, z - 3),
+        (y >= 1, own, near.at[0], 1, 0, z - 1),
+        ((y == 0) & has_prev, own, passing, 2, 3, z + 3),
+    ]
+    pass_sends = [((y == LINE - 1) & has_prev, passing, near.at[0], 3, 0, z - LINE)]
+    first_sends = [(relays, near.at[0], near.at[1], 4, 1, z - 1)]
+    third_sends = [(relays & has_next, near.at[2], near.at[1], 5, 1, z + 1)]
+    all_sends = own_sends + pass_sends + first_sends + third_sends
+
+    def send_all(sends, c):
+        for condition, src, dst, send, slot, gz in sends:
+
+            @pl.when(condition)
+            def _():
+                patch_copy(src, dst, send, slot, c, gz).start()
+
+    def arrived(slot, c):
+        buffer = passing if slot == 3 else near.at[slot]
+        patch_copy(buffer, buffer, 0, slot, c, z).wait_recv()
+
+    exchange_start(0)
+    for k in range(1, 4):
+
+        @pl.when(z + k < depth)
+        def _():
+            w_copy(k).start()
+
+    def send_own(c, carry):
+        send_all(own_sends, c)
+        return carry
+
+    lax.fori_loop(0, AHEAD, send_own, 0)
 
     row_id = lax.broadcasted_iota(jnp.int32, (16, length), 0)
     row_id = jnp.where(row_id < 8, row_id, row_id - 16)
@@ -339,10 +361,10 @@
             value = jnp.where((tap_row == 2 * q + r) & (tap_col == c), sums[q], value)
         taps[k] = value
 
-    def correlate(k, c):
-        def body(i, carry):
-            p = c * piece + 2 * i
-            s = spectra(near.at[k], p)
+    def correlate(works):
+        pairs = [(k, c * piece + 2 * i) for i in range(piece // 2) for k, c in works]
+        crossed = []
+        for (k, p), s in zip(pairs, spectra([(near.at[k], p) for k, p in pairs])):
             mixed = []
             for a in range(2):
                 cols = slice(a * half, (a + 1) * half)
@@ -351,56 +373,76 @@
                 real = (a_real * b_real + a_imag * b_imag).astype(BF16)
                 imag = (a_real * b_imag - a_imag * b_real).astype(BF16)
                 mixed.append(jnp.concatenate([real, imag], axis=1))
-            halves = dot(jnp.concatenate(mixed, axis=0), back[...]).astype(BF16)
-            corr = dot(last[...], side_by_side(halves)) * (1.0 / (length * length))
+            crossed.append(jnp.concatenate(mixed, axis=0))
+        halves = [dot(m, back[...]).astype(BF16) for m in crossed]
+        corrs = [dot(last[...], side_by_side(h)) * (1.0 / (length * length)) for h in halves]
+        for (k, p), corr in zip(pairs, corrs):
             for a in range(2):
                 one = corr[:, a * half : (a + 1) * half]
                 staged[k, p + a] = one.astype(BF16)
                 pick(k, p + a, jnp.concatenate([one[:8], one[length - 8 :]], axis=0))
-            return carry
-
-        lax.fori_loop(0, piece // 2, body, 0)
-        part = part_of(c)
-        pltpu.make_async_copy(staged.at[k, part], surfaces.at[k, part], surf_sem).start()
+        for k, c in works:
+            part = part_of(c)
+            pltpu.make_async_copy(staged.at[k, part], surfaces.at[k, part], surf_sem).start()
+
+    late = jnp.where(y == LINE - 1, LAG, 0)
 
     def step(c, carry):
+        @pl.when(c < CHUNKS - AHEAD)
+        def _():
+            send_own(c + AHEAD, 0)
+
+        c_0 = c - late
+        c_1 = c - LAG
+        has_0 = (c_0 >= 0) & (c_0 < CHUNKS)
+
         @pl.when(c < CHUNKS)
         def _():
-            own_spectra(c)
-
+            @pl.when((y == LINE - 1) & has_prev)
+            def _():
+                arrived(3, c)
+
+            send_all(pass_sends, c)
+
+            @pl.when(z + 3 < depth)
+            def _():
+                arrived(2, c)
+
+            send_all(third_sends, c)
+
+        @pl.when(has_0)
+        def _():
             @pl.when(z + 1 < depth)
             def _():
-                arrived(0, c)
-
-            send_all(first_sends, c)
-
-            @pl.when((y < LINE - 1) & has_next)
-            def _():
-                arrived(3, c)
-
-            send_all(cross_sends, c)
-            correlate(0, c)
-
-        @pl.when((c >= 1) & (c < CHUNKS + 1))
-        def _():
-            @pl.when(z + 3 < depth)
-            def _():
-                arrived(2, c - 1)
-
-            send_all(third_sends, c - 1)
-            correlate(2, c - 1)
-
-        @pl.when(c >= 2)
-        def _():
-            @pl.when(z + 2 < depth)
-            def _():
-                arrived(1, c - 2)
-
-            correlate(1, c - 2)
+                arrived(0, c_0)
+
+            send_all(first_sends, c_0)
+
+        @pl.when((c_1 >= 0) & (z + 2 < depth))
+        def _():
+            arrived(1, c_1)
+
+        steady = (c_1 >= 0) & (c < CHUNKS)
+
+        @pl.when(steady)
+        def _():
+            correlate([(2, c), (0, c_0), (1, c_1)])
+
+        @pl.when(jnp.logical_not(steady) & (c < CHUNKS))
+        def _():
+            correlate([(2, c)])
+
+        @pl.when(jnp.logical_not(steady) & has_0)
+        def _():
+            correlate([(0, c_0)])
+
+        @pl.when(jnp.logical_not(steady) & (c_1 >= 0))
+        def _():
+            correlate([(1, c_1)])
 
         return carry
 
-    lax.fori_loop(0, CHUNKS + 2, step, 0)
+    lax.fori_loop(0, CHUNKS + LAG, step, 0)
 
     for k in range(1, 4):
         sums = taps[k - 1]
@@ -493,12 +535,17 @@
     def group_copy(i):
         other = lax.rem(me + i, group)
         return remote(
-            gram, gram_a.at[me], gs.at[0, i], gr.at[0, i], line * LINE + lax.div(other, tiles), lax.rem(other, tiles)
+            gram_row.at[0],
+            gram_a.at[me],
+            gs.at[0, i],
+            gr.at[0, i],
+            line * LINE + lax.div(other, tiles),
+            lax.rem(other, tiles),
         )
 
     def lines_copy(i):
         other = lax.rem(line + i, lines)
-        return remote(gram, gram_b.at[line], gs.at[1, i], gr.at[1, i], other * LINE + y, t)
+        return remote(gram_row.at[1], gram_b.at[line], gs.at[1, i], gr.at[1, i], other * LINE + y, t)
 
     def run(copy, number, what):
         def body(i, carry):
@@ -509,25 +556,68 @@
 
     for n in range(len(PAIRS), gram.shape[0]):
         gram[n : n + 1] = jnp.zeros((1, length), F32)
+    summed = jnp.sum(gram[...], axis=1, keepdims=True)
+    on_row = lax.broadcasted_iota(jnp.int32, gram.shape, 0) == lax.broadcasted_iota(jnp.int32, gram.shape, 1)
+    mine = jnp.sum(jnp.where(on_row, summed, 0.0), axis=0, keepdims=True)
+    gram_row[0] = mine
     run(group_copy, group, "start")
-    gram_a[me] = gram[...]
+    gram_a[me] = mine
     run(group_copy, group, "wait")
     total = gram_a[0]
     for i in range(1, group):
         total = total + gram_a[i]
-    gram[...] = total
+    gram_row[1] = total
     run(lines_copy, lines, "start")
     gram_b[line] = total
     run(lines_copy, lines, "wait")
     total = gram_b[0]
     for i in range(1, lines):
         total = total + gram_b[i]
-    total = jnp.broadcast_to(jnp.sum(total, axis=1, keepdims=True), total.shape)
+    gram_out[...] = jnp.broadcast_to(jnp.sum(jnp.where(on_row, total, 0.0), axis=1, keepdims=True), gram.shape)
+
+    for k in range(1, 4):
+
+        @pl.when(z + k < depth)
+        def _():
+            w_copy(k).wait_send()
+            t_copy(k).wait_send()
+
+    for r in range(ITERS):
+        exchange_drain(r)
+    for condition, src, dst, send, slot, gz in all_sends:
+
+        @pl.when(condition)
+        def _():
+            remote(src, dst, ps.at[send], pr.at[slot, 0], gz, t).wait_send()
+
+    pltpu.make_async_copy(staged, surfaces, surf_sem).wait()
+
+
+def finish(number, start_h, fields_h, gram_h, targets_h, staged, positions, targets, surfaces, norms, held, start, fields, gram, sem_in, sem_out, sem):
+    ways = [
+        pltpu.make_async_copy(source, to, sem.at[n])
+        for n, (source, to) in enumerate(((gram_h, gram), (start_h, start), (fields_h, fields), (targets_h, targets)))
+    ]
+    for copy in ways:
+        copy.start()
+    pieces = held.shape[0] // 4
+    inward, outward = [], []
+    for n in range(4):
+        part = pl.ds(n * pieces, pieces)
+        inward.append(pltpu.make_async_copy(staged.at[part], held.at[part], sem_in.at[n]))
+        outward.append(pltpu.make_async_copy(held.at[part], surfaces.at[part], sem_out.at[n]))
+        inward[n].start()
+    for copy in ways:
+        copy.wait()
+    for n in range(4):
+        inward[n].wait()
+        outward[n].start()
+    length = gram.shape[1]
+    total = gram[...]
 
     entries = {}
     for n, (first, second) in enumerate(PAIRS):
         entries[first, second] = entries[second, first] = total[n : n + 1]
-    number = 2.0 * depth * tiles * nodes_rows * nodes_cols
     ones = jnp.ones((1, length), F32)
     coefficients = [ones]
     sums = [jnp.zeros((1, length), F32)] * ITERS
@@ -537,7 +627,7 @@
             for second in range(len(coefficients)):
                 square = square + coefficients[first] * coefficients[second] * entries[first, second]
         rms = jnp.sqrt(jnp.maximum(square, 0.0) / number + tiny_eps)
-        norms[i : i + 1] = rms
+        norms[i] = rms[0, 0]
         factor = jnp.minimum(1.0, clip_level / rms)
         for n in range(len(coefficients)):
             sums[n] = sums[n] + step_size * factor * coefficients[n]
@@ -549,23 +639,8 @@
         for n in range(ITERS):
             result = result + jnp.concatenate([sums[n], sums[n]], axis=1) * fields[n, a]
         positions[a] = result
-
-    for k in range(1, 4):
-
-        @pl.when(z + k < depth)
-        def _():
-            w_copy(k).wait_send()
-            t_copy(k).wait_send()
-
-    for r in range(ITERS):
-        exchange_drain(r)
-    for condition, src, dst, send, slot, gz in all_sends:
-
-        @pl.when(condition)
-        def _():
-            remote(src, dst, ps.at[send], pr.at[slot, 0], gz, t).wait_send()
-
-    pltpu.make_async_copy(staged, surfaces, surf_sem).wait()
+    for copy in outward:
+        copy.wait()
 
 
 def local(depth, tiles, patches, peak_offsets, valid_masks, initial_positions):
@@ -575,21 +650,22 @@
     offsets = peak_offsets.reshape(6, rows_dev, columns)
     vmem = pl.BlockSpec(memory_space=pltpu.VMEM)
     smem = pl.BlockSpec(memory_space=pltpu.SMEM)
-    hbm = pl.BlockSpec(memory_space=pl.ANY)
+    hbm = pl.BlockSpec(memory_space=pltpu.HBM)
     group = LINE * tiles
     lines = depth // LINE
     dma = pltpu.SemaphoreType.DMA
     flops = 2 * count * (4 * 6 + 3 * 6) * length**3
-    outs = pl.pallas_call(
+    start = initial_positions.reshape(2, nodes_rows, nodes_cols)
+    targets, staged, fields, gram = pl.pallas_call(
         functools.partial(kernel, depth, tiles),
         out_shape=(
-            jax.ShapeDtypeStruct((2, nodes_rows, nodes_cols), F32),
             jax.ShapeDtypeStruct((6, rows_dev, columns), F32),
             jax.ShapeDtypeStruct((3, count, length, length), BF16),
-            jax.ShapeDtypeStruct((ITERS, length), F32),
+            jax.ShapeDtypeStruct((ITERS, 2, nodes_rows, nodes_cols), F32),
+            jax.ShapeDtypeStruct((16, length), F32),
         ),
-        in_specs=[hbm, smem, vmem, vmem, vmem, vmem, vmem, vmem, vmem],
-        out_specs=(vmem, vmem, hbm, vmem),
+        in_specs=[hbm, hbm, hbm, hbm, hbm],
+        out_specs=(vmem, hbm, vmem, vmem),
         scratch_shapes=[
             pltpu.VMEM((count, length, length), BF16),
             pltpu.VMEM((3, count, length, length), BF16),
@@ -597,6 +673,11 @@
             pltpu.VMEM((count, length, length), F32),
             pltpu.VMEM((count, length, length), F32),
             pltpu.VMEM((3, count, length, length), BF16),
+            pltpu.SMEM((6, rows_dev, columns), jnp.int32),
+            pltpu.VMEM((6, rows_dev, columns), jnp.int32),
+            pltpu.VMEM((3, rows_dev, columns), jnp.int32),
+            pltpu.VMEM((2, nodes_rows, nodes_cols), F32),
+            pltpu.VMEM((6 * length, 2 * length), BF16),
             pltpu.VMEM((3, 8, length), F32),
             pltpu.VMEM((ITERS, 2, nodes_rows, nodes_cols), BF16),
             pltpu.VMEM((ITERS, 6, 2, nodes_rows, nodes_cols), BF16),
@@ -607,13 +688,14 @@
             pltpu.VMEM((3, 8, length), F32),
             pltpu.VMEM((3, 8, length), F32),
             pltpu.VMEM((6, nodes_rows, nodes_cols), F32),
-            pltpu.VMEM((ITERS, 2, nodes_rows, nodes_cols), F32),
             pltpu.VMEM((16, length), F32),
-            pltpu.VMEM((group, 16, length), F32),
-            pltpu.VMEM((lines, 16, length), F32),
+            pltpu.VMEM((2, 1, length), F32),
+            pltpu.VMEM((group, 1, length), F32),
+            pltpu.VMEM((lines, 1, length), F32),
             dma((CHUNKS,)),
+            dma((5,)),
             dma,
-            dma((7,)),
+            dma((6,)),
             dma((4, CHUNKS)),
             dma((ITERS, 6)),
             dma((ITERS, 6)),
@@ -631,17 +713,36 @@
     )(
         patches.reshape(count, length, length),
         offsets,
-        offsets,
         valid_masks.reshape(3, rows_dev, columns),
-        initial_positions.reshape(2, nodes_rows, nodes_cols),
-        *[jnp.asarray(table) for table in tables(length)],
+        start,
+        jnp.asarray(tables(length)),
     )
-    positions, targets, surfaces, norms = outs
+    number = 2.0 * depth * tiles * nodes_rows * nodes_cols
+    positions, targets, surfaces, norms = pl.pallas_call(
+        functools.partial(finish, number),
+        out_shape=(
+            jax.ShapeDtypeStruct((2, nodes_rows, nodes_cols), F32),
+            jax.ShapeDtypeStruct((6, rows_dev, columns), F32),
+            jax.ShapeDtypeStruct((3 * count, length, length), BF16),
+            jax.ShapeDtypeStruct((ITERS,), F32),
+        ),
+        in_specs=[hbm, hbm, hbm, hbm, hbm],
+        out_specs=(vmem, vmem, hbm, smem),
+        scratch_shapes=[
+            pltpu.VMEM((3 * count, length, length), BF16),
+            pltpu.VMEM((2, nodes_rows, nodes_cols), F32),
+            pltpu.VMEM((ITERS, 2, nodes_rows, nodes_cols), F32),
+            pltpu.VMEM((16, length), F32),
+            dma((4,)),
+            dma((4,)),
+            dma((4,)),
+        ],
+    )(start, fields, gram, targets, staged.reshape(3 * count, length, length))
     return (
         positions.reshape(initial_positions.shape),
         targets.reshape(peak_offsets.shape),
         surfaces.reshape(1, 3, rows_dev, columns, length, length),
-        norms[:, 0],
+        norms,
     )
 
 

time: 137 us -> 118 us (0.86)
  Pallas kernels: 128 us -> 117 us
  local copies, waits for them, and re-layouts: 8.01 us -> 0 us
    pallas_call x1, Pallas kernels: 128 us -> 113 us  [local(): pl.pallas_call(functools.partial(kernel, depth, tiles), out_shape=(jax.Sh...]
    unnamed x3 -> x0, local copies, waits for them, and re-layouts: 6.72 us -> none
    pallas_call x0 -> x1, Pallas kernels: none -> 3.92 us  [local(): pl.pallas_call(functools.partial(finish, number), out_shape=(jax.ShapeDty...]
where the time goes in v2:
time: 118 us
  Pallas kernels  117 us (99%)
    pallas_call x1, Pallas kernels, local(): pl.pallas_call(functools.partial(kernel, depth, tiles), out_shape=(jax.Sh...  113 us
    pallas_call x1, Pallas kernels, local(): pl.pallas_call(functools.partial(finish, number), out_shape=(jax.ShapeDty...  3.92 us

profile of v2, /device:TPU:1, one launch (start us, length us, event | category | flops | bytes accessed | tf_op | source)
XLA Modules:
  0.0 118.0 jit_solution(16080161237671476780)
XLA Ops:
  0.6 113.4 %shard_map.84 = (f32[6,2,16]{2,1,0:T(2,128)}, bf16[3,32,128,128]{3,2,1,0:T(8,128)(2,1)}, f32[4,2,32,256]{3,2,1,0:T(8,128)}, f32[16,128]{1,0:T(8,128)}) custom-call(bf16[32,128,128]{2,1,0:T(8,128)(2,1)} %bitcast.14, s32[6,2,16]{2,1,0:T(2,128)} %bitcast.16, s32[3,2,16]{2,1,0:T(2,128)} %bitcast.18, f32[2,32,256]{2,1,0:T(8,128)} %bitcast.11, ...), custom_call_target="tpu_custom_call" | custom-call | flops 5637144576 | bytes 5242880 | tf_op jit(solution)/shard_map/pallas_call | solution.py:659
  114.0 3.9 %shard_map.85 = (f32[2,32,256]{2,1,0:T(8,128)}, f32[6,2,16]{2,1,0:T(2,128)}, bf16[96,128,128]{2,1,0:T(8,128)(2,1)}, f32[4]{0:T(128)}) custom-call(f32[2,32,256]{2,1,0:T(8,128)} %bitcast.12, f32[4,2,32,256]{3,2,1,0:T(8,128)} %get-tuple-element.12.fields_h, f32[16,128]{1,0:T(8,128)} %get-tuple-element.13.gram_h, f32[6,2,16]{2,1,0:T(2,128)} %get-tuple-element.14.targets_h, ...), custom_call_target="tpu_custom_call" | custom-call | tf_op jit(solution)/shard_map/pallas_call | solution.py:721

commit v3 on v2

--- a/solution.py
+++ b/solution.py
@@ -319,7 +319,6 @@
         buffer = passing if slot == 3 else near.at[slot]
         patch_copy(buffer, buffer, 0, slot, c, z).wait_recv()
 
-    exchange_start(0)
     for k in range(1, 4):
 
         @pl.when(z + k < depth)
@@ -391,6 +390,10 @@
         @pl.when(c < CHUNKS - AHEAD)
         def _():
             send_own(c + AHEAD, 0)
+
+        @pl.when(c == 14)
+        def _():
+            exchange_start(0)
 
         c_0 = c - late
         c_1 = c - LAG

time: 118 us -> 116 us (0.983)
  Pallas kernels: 117 us -> 115 us
    pallas_call x1, Pallas kernels: 113 us -> 112 us  [local(): pl.pallas_call(functools.partial(kernel, depth, tiles), out_shape=(jax.Sh...]
where the time goes in v3:
time: 116 us
  Pallas kernels  115 us (99%)
    pallas_call x1, Pallas kernels, local(): pl.pallas_call(functools.partial(kernel, depth, tiles), out_shape=(jax.Sh...  112 us
    pallas_call x1, Pallas kernels, local(): pl.pallas_call(functools.partial(finish, number), out_shape=(jax.ShapeDty...  3.92 us

profile of v3, /device:TPU:1, one launch (start us, length us, event | category | flops | bytes accessed | tf_op | source)
XLA Modules:
  0.0 116.1 jit_solution(10869147707618591133)
XLA Ops:
  0.6 111.5 %shard_map.84 = (f32[6,2,16]{2,1,0:T(2,128)}, bf16[3,32,128,128]{3,2,1,0:T(8,128)(2,1)}, f32[4,2,32,256]{3,2,1,0:T(8,128)}, f32[16,128]{1,0:T(8,128)}) custom-call(bf16[32,128,128]{2,1,0:T(8,128)(2,1)} %bitcast.14, s32[6,2,16]{2,1,0:T(2,128)} %bitcast.16, s32[3,2,16]{2,1,0:T(2,128)} %bitcast.18, f32[2,32,256]{2,1,0:T(8,128)} %bitcast.11, ...), custom_call_target="tpu_custom_call" | custom-call | flops 5637144576 | bytes 5242880 | tf_op jit(solution)/shard_map/pallas_call | solution.py:662
  112.2 3.9 %shard_map.85 = (f32[2,32,256]{2,1,0:T(8,128)}, f32[6,2,16]{2,1,0:T(2,128)}, bf16[96,128,128]{2,1,0:T(8,128)(2,1)}, f32[4]{0:T(128)}) custom-call(f32[2,32,256]{2,1,0:T(8,128)} %bitcast.12, f32[4,2,32,256]{3,2,1,0:T(8,128)} %get-tuple-element.12.fields_h, f32[16,128]{1,0:T(8,128)} %get-tuple-element.13.gram_h, f32[6,2,16]{2,1,0:T(2,128)} %get-tuple-element.14.targets_h, ...), custom_call_target="tpu_custom_call" | custom-call | tf_op jit(solution)/shard_map/pallas_call | solution.py:724

commit v4 on v3

--- a/solution.py
+++ b/solution.py
@@ -13,7 +13,8 @@
 ITERS = 4
 LINE = 4
 CHUNKS = 16
-AHEAD = 4
+AHEAD = 6
+FAR_AHEAD = 3
 OWN_STEP = 8
 LAG = 2
 
@@ -298,15 +299,15 @@
         return remote(src.at[part], dst.at[part], ps.at[send], pr.at[slot, c], gz, t)
 
     relays = (y == 1) | (y == 2)
-    own_sends = [
+    far_sends = [
         (z >= 3, own, near.at[2], 0, 2, z - 3),
-        (y >= 1, own, near.at[0], 1, 0, z - 1),
         ((y == 0) & has_prev, own, passing, 2, 3, z + 3),
     ]
+    next_sends = [(y >= 1, own, near.at[0], 1, 0, z - 1)]
     pass_sends = [((y == LINE - 1) & has_prev, passing, near.at[0], 3, 0, z - LINE)]
     first_sends = [(relays, near.at[0], near.at[1], 4, 1, z - 1)]
     third_sends = [(relays & has_next, near.at[2], near.at[1], 5, 1, z + 1)]
-    all_sends = own_sends + pass_sends + first_sends + third_sends
+    all_sends = far_sends + next_sends + pass_sends + first_sends + third_sends
 
     def send_all(sends, c):
         for condition, src, dst, send, slot, gz in sends:
@@ -325,11 +326,16 @@
         def _():
             w_copy(k).start()
 
-    def send_own(c, carry):
-        send_all(own_sends, c)
+    def send_far(c, carry):
+        send_all(far_sends, c)
         return carry
 
-    lax.fori_loop(0, AHEAD, send_own, 0)
+    def send_next(c, carry):
+        send_all(next_sends, c)
+        return carry
+
+    lax.fori_loop(0, AHEAD, send_next, 0)
+    lax.fori_loop(0, FAR_AHEAD, send_far, 0)
 
     row_id = lax.broadcasted_iota(jnp.int32, (16, length), 0)
     row_id = jnp.where(row_id < 8, row_id, row_id - 16)
@@ -387,11 +393,15 @@
     late = jnp.where(y == LINE - 1, LAG, 0)
 
     def step(c, carry):
+        @pl.when(c < CHUNKS - FAR_AHEAD)
+        def _():
+            send_far(c + FAR_AHEAD, 0)
+
         @pl.when(c < CHUNKS - AHEAD)
         def _():
-            send_own(c + AHEAD, 0)
-
-        @pl.when(c == 14)
+            send_next(c + AHEAD, 0)
+
+        @pl.when(c == CHUNKS)
         def _():
             exchange_start(0)
 

time: 116 us -> 114 us (0.983)
  Pallas kernels: 115 us -> 113 us
    pallas_call x1, Pallas kernels: 112 us -> 109 us  [local(): pl.pallas_call(functools.partial(kernel, depth, tiles), out_shape=(jax.Sh...]
where the time goes in v4:
time: 114 us
  Pallas kernels  113 us (99%)
    pallas_call x1, Pallas kernels, local(): pl.pallas_call(functools.partial(kernel, depth, tiles), out_shape=(jax.Sh...  109 us
    pallas_call x1, Pallas kernels, local(): pl.pallas_call(functools.partial(finish, number), out_shape=(jax.ShapeDty...  3.92 us

profile of v4, /device:TPU:1, one launch (start us, length us, event | category | flops | bytes accessed | tf_op | source)
XLA Modules:
  0.0 113.9 jit_solution(10524778339253668181)
XLA Ops:
  0.6 109.4 %shard_map.84 = (f32[6,2,16]{2,1,0:T(2,128)}, bf16[3,32,128,128]{3,2,1,0:T(8,128)(2,1)}, f32[4,2,32,256]{3,2,1,0:T(8,128)}, f32[16,128]{1,0:T(8,128)}) custom-call(bf16[32,128,128]{2,1,0:T(8,128)(2,1)} %bitcast.14, s32[6,2,16]{2,1,0:T(2,128)} %bitcast.16, s32[3,2,16]{2,1,0:T(2,128)} %bitcast.18, f32[2,32,256]{2,1,0:T(8,128)} %bitcast.11, ...), custom_call_target="tpu_custom_call" | custom-call | flops 5637144576 | bytes 5242880 | tf_op jit(solution)/shard_map/pallas_call | solution.py:672
  110.0 3.9 %shard_map.85 = (f32[2,32,256]{2,1,0:T(8,128)}, f32[6,2,16]{2,1,0:T(2,128)}, bf16[96,128,128]{2,1,0:T(8,128)(2,1)}, f32[4]{0:T(128)}) custom-call(f32[2,32,256]{2,1,0:T(8,128)} %bitcast.12, f32[4,2,32,256]{3,2,1,0:T(8,128)} %get-tuple-element.12.fields_h, f32[16,128]{1,0:T(8,128)} %get-tuple-element.13.gram_h, f32[6,2,16]{2,1,0:T(2,128)} %get-tuple-element.14.targets_h, ...), custom_call_target="tpu_custom_call" | custom-call | tf_op jit(solution)/shard_map/pallas_call | solution.py:734

commit v5 on v4

--- a/solution.py
+++ b/solution.py
@@ -13,7 +13,7 @@
 ITERS = 4
 LINE = 4
 CHUNKS = 16
-AHEAD = 6
+AHEAD = 8
 FAR_AHEAD = 3
 OWN_STEP = 8
 LAG = 2

time: 114 us -> 114 us (level)
  no operation moved by 1% of the time
where the time goes in v5:
time: 114 us
  Pallas kernels  113 us (99%)
    pallas_call x1, Pallas kernels, local(): pl.pallas_call(functools.partial(kernel, depth, tiles), out_shape=(jax.Sh...  109 us
    pallas_call x1, Pallas kernels, local(): pl.pallas_call(functools.partial(finish, number), out_shape=(jax.ShapeDty...  3.92 us

profile of v5, /device:TPU:1, one launch (start us, length us, event | category | flops | bytes accessed | tf_op | source)
XLA Modules:
  0.0 113.6 jit_solution(9492588990405076577)
XLA Ops:
  0.6 109.1 %shard_map.84 = (f32[6,2,16]{2,1,0:T(2,128)}, bf16[3,32,128,128]{3,2,1,0:T(8,128)(2,1)}, f32[4,2,32,256]{3,2,1,0:T(8,128)}, f32[16,128]{1,0:T(8,128)}) custom-call(bf16[32,128,128]{2,1,0:T(8,128)(2,1)} %bitcast.14, s32[6,2,16]{2,1,0:T(2,128)} %bitcast.16, s32[3,2,16]{2,1,0:T(2,128)} %bitcast.18, f32[2,32,256]{2,1,0:T(8,128)} %bitcast.11, ...), custom_call_target="tpu_custom_call" | custom-call | flops 5637144576 | bytes 5242880 | tf_op jit(solution)/shard_map/pallas_call | solution.py:672
  109.7 3.9 %shard_map.85 = (f32[2,32,256]{2,1,0:T(8,128)}, f32[6,2,16]{2,1,0:T(2,128)}, bf16[96,128,128]{2,1,0:T(8,128)(2,1)}, f32[4]{0:T(128)}) custom-call(f32[2,32,256]{2,1,0:T(8,128)} %bitcast.12, f32[4,2,32,256]{3,2,1,0:T(8,128)} %get-tuple-element.12.fields_h, f32[16,128]{1,0:T(8,128)} %get-tuple-element.13.gram_h, f32[6,2,16]{2,1,0:T(2,128)} %get-tuple-element.14.targets_h, ...), custom_call_target="tpu_custom_call" | custom-call | tf_op jit(solution)/shard_map/pallas_call | solution.py:734
